TPU v7x, 32 devices: a 4x4x1 block of a 4x4x8 slice. The times are simulated.
32 devices in a mesh: rep: 1 (over z), dp: 32 (over x, y, core).
Axes of the slice: x: 4, y: 4, z: 1, core: 2. Of those that a mesh axis runs over, the one named last changes fastest.
The devices are a block of a 4x4x8 slice.
Arguments:
- x: bfloat16 [32, 2048, 896], P(('rep', 'dp'))
- dy: bfloat16 [32, 2048, 896], P(('rep', 'dp'))
- w_gate: bfloat16 [2, 896, 2560], P(None, 'dp')
- w_up: bfloat16 [2, 896, 2560], P(None, 'dp')
- w_down: bfloat16 [2, 2560, 896], P(None, 'dp')
Outputs:
- output 1: bfloat16 [32, 2048, 896], P(('rep', 'dp'))
- output 2: bfloat16 [2, 896, 2560], P('rep', 'dp')
- output 3: bfloat16 [2, 896, 2560], P('rep', 'dp')
- output 4: bfloat16 [2, 2560, 896], P('rep', 'dp')
All inputs are finite; a program needn't handle non-finite values.
Results may differ from a plain program's by a relative error of at most 0.018.
Values are sent between devices in bfloat16 or wider.
A program may use at most 768 MiB of HBM per device.

v0:
```python
import jax
import jax.numpy as jnp
from jax import lax

NAMES = ("w_gate", "w_up", "w_down")


def matmul(a, w):
    return jnp.dot(a, w, preferred_element_type=jnp.float32).astype(jnp.bfloat16)


def normed(h):
    wide = h.astype(jnp.float32)
    scale = lax.rsqrt(jnp.mean(wide**2, -1, keepdims=True) + 1e-6)
    return (wide * scale).astype(jnp.bfloat16)


def layer(h, w):
    a = normed(h)
    gate = jnp.dot(a, w["w_gate"], preferred_element_type=jnp.float32)
    up = jnp.dot(a, w["w_up"], preferred_element_type=jnp.float32)
    return h + matmul((jax.nn.silu(gate) * up).astype(jnp.bfloat16), w["w_down"])


def stack(weights, h):
    for number in range(weights["w_gate"].shape[0]):
        h = layer(h, {name: w[number] for name, w in weights.items()})
    return h


def solution(mesh):
    groups = mesh.shape["rep"]

    def step(x, dy, *weights):
        shape = x.shape
        x, dy = (t.reshape(groups, -1, *t.shape[1:]) for t in (x, dy))

        def of_a_group(x, dy):
            _, back = jax.vjp(stack, dict(zip(NAMES, weights, strict=True)), x)
            by_weights, by_x = back(dy)
            return (by_x, *(by_weights[name] for name in NAMES))

        by_x, *by_weights = jax.vmap(of_a_group)(x, dy)
        return (by_x.reshape(shape), *(t.reshape(-1, *t.shape[2:]) for t in by_weights))

    return step
```

profile of v0, /device:TPU:97, one launch (start us, length us, event | category | flops | bytes accessed | tf_op | source)
XLA Modules:
  0.0 1024.3 jit_solution(2592715053259759576)
XLA Ops:
  31.7 32.0 %all-gather.30.cloned.1.call-done = bf16[1,896,2560]{2,0,1:T(2,128)(2,1)} async-done(((bf16[1,28,2560]{2,0,1:T(2,128)(2,1)}), bf16[1,896,2560]{2,0,1:T(2,128)(2,1)}) %all-gather.30.cloned.1.call-update) | async-done | bytes 4587536 | tf_op jit(solution)/vmap(jvp())/squeeze | solution.py:27
  63.6 19.0 %fusion.58 = f32[2048,2560]{1,0:T(8,128)} fusion(bf16[1,2048,896]{1,2,0:T(8,128)(2,1)} %copy.17, f32[2048]{0:T(1024)S(1)} %bitcast.269, bf16[1,896,2560]{2,0,1:T(2,128)(2,1)} %all-gather.30.cloned.1.call-done), kind=kOutput, calls=%fused_computation.75 | convolution fusion | flops 9400745984 | bytes 29237248 | tf_op jit(solution)/vmap(jvp())/dot_general | solution.py:20
  82.6 32.5 %all-gather.32.cloned.1.call-done = bf16[1,896,2560]{2,0,1:T(2,128)(2,1)} async-done(((bf16[1,28,2560]{2,0,1:T(2,128)(2,1)}), bf16[1,896,2560]{2,0,1:T(2,128)(2,1)}) %all-gather.32.cloned.1.call-update) | async-done | bytes 4587536 | tf_op jit(solution)/vmap(jvp())/squeeze | solution.py:27
  115.1 19.1 %fusion.54 = f32[2048,2560]{1,0:T(8,128)} fusion(bf16[1,2048,896]{1,2,0:T(8,128)(2,1)} %copy.17, f32[2048]{0:T(1024)S(1)} %bitcast.270, bf16[1,896,2560]{2,0,1:T(2,128)(2,1)} %all-gather.32.cloned.1.call-done), kind=kOutput, calls=%fused_computation.71 | convolution fusion | flops 9400745984 | bytes 29237248 | tf_op jit(solution)/vmap(jvp())/dot_general | solution.py:21
  134.2 19.4 %fusion.28 = bf16[2048,2560]{1,0:T(8,128)(2,1)} fusion(f32[2048,2560]{1,0:T(8,128)} %fusion.54, f32[2048,2560]{1,0:T(8,128)} %fusion.58), kind=kLoop, calls=%fused_computation.44 | loop fusion | flops 31457280 | bytes 52428800
  158.2 16.4 %fusion.43 = (f32[2048]{0:T(1024)S(1)}, bf16[1,2048,896]{1,2,0:T(8,128)(2,1)}) fusion(bf16[1,2048,896]{1,2,0:T(8,128)(2,1)} %copy.17, bf16[2048,2560]{1,0:T(8,128)(2,1)} %fusion.28, bf16[1,2560,896]{2,1,0:T(8,128)(2,1)} %all-gather.34.cloned.1.call-done), kind=kOutput, calls=%fused_computation.60 | convolution fusion | flops 9404413952 | bytes 22421504 | tf_op jit(solution)/vmap(jvp())/dot_general | solution.py:9
  175.2 25.8 %all-gather.38.cloned.1.call-done = bf16[1,2560,896]{2,1,0:T(8,128)(2,1)} async-done(((bf16[1,80,896]{2,1,0:T(8,128)(2,1)}), bf16[1,2560,896]{2,1,0:T(8,128)(2,1)}) %all-gather.38.cloned.1.call-update) | async-done | bytes 4587536 | tf_op jit(solution)/vmap(jvp())/squeeze | solution.py:27
  200.9 16.5 %convolution_convert_fusion.1 = bf16[2048,2560]{1,0:T(8,128)(2,1)} fusion(bf16[1,2560,896]{2,1,0:T(8,128)(2,1)} %all-gather.38.cloned.1.call-done, bf16[1,2048,896]{2,1,0:T(8,128)(2,1)} %param), kind=kOutput, calls=%fused_computation.43 | convolution fusion | flops 9400483840 | bytes 18743296 | tf_op jit(solution)/vmap(transpose(jvp()))/dot_general | solution.py:9
  217.4 34.6 %all-gather.36.cloned.1.call-done = bf16[1,896,2560]{2,0,1:T(2,128)(2,1)} async-done(((bf16[1,28,2560]{2,0,1:T(2,128)(2,1)}), bf16[1,896,2560]{2,0,1:T(2,128)(2,1)}) %all-gather.36.cloned.1.call-update) | async-done | bytes 4587536 | tf_op jit(solution)/vmap(jvp())/squeeze | solution.py:27
  252.0 19.3 %fusion.51 = f32[2048,2560]{1,0:T(8,128)} fusion(bf16[1,2048,896]{1,2,0:T(8,128)(2,1)} %get-tuple-element.31, f32[2048]{0:T(1024)S(1)} %bitcast.274, bf16[1,896,2560]{2,0,1:T(2,128)(2,1)} %all-gather.36.cloned.1.call-done), kind=kOutput, calls=%fused_computation.68 | convolution fusion | flops 9400745984 | bytes 29237248 | tf_op jit(solution)/vmap(jvp())/dot_general | solution.py:20
  271.4 19.1 %fusion.24 = f32[2560,896]{0,1:T(8,128)} fusion(bf16[2048,2560]{1,0:T(8,128)(2,1)} %convolution_convert_fusion.1, f32[2048,2560]{1,0:T(8,128)} %fusion.51, bf16[1,2048,896]{1,2,0:T(8,128)(2,1)} %get-tuple-element.31, f32[2048]{0:T(1024)S(1)} %bitcast.275), kind=kOutput, calls=%fused_computation.32 | convolution fusion | flops 9432203264 | bytes 44310528 | tf_op jit(solution)/vmap(transpose(jvp()))/dot_general | solution.py:21
  290.4 91.6 %fusion.2 = f32[2560,32]{0,1:T(8,128)S(1)} fusion(f32[2560,896]{0,1:T(8,128)} %fusion.24), kind=kCustom, calls=%all-reduce-scatter.2 | all-reduce-scatter fusion | flops 2621441 | bytes 9502720
  389.6 18.9 %fusion.46 = f32[2048,2560]{1,0:T(8,128)} fusion(bf16[1,2048,896]{1,2,0:T(8,128)(2,1)} %get-tuple-element.31, f32[2048]{0:T(1024)S(1)} %bitcast.276, bf16[1,896,2560]{2,0,1:T(2,128)(2,1)} %all-gather.40.cloned.1.call-done), kind=kOutput, calls=%fused_computation.63 | convolution fusion | flops 9400745984 | bytes 29237248 | tf_op jit(solution)/vmap(jvp())/dot_general | solution.py:21
  408.5 18.2 %fusion.8 = bf16[2048,2560]{1,0:T(8,128)(2,1)S(1)} fusion(f32[2048,2560]{1,0:T(8,128)} %fusion.51, f32[2048,2560]{1,0:T(8,128)} %fusion.46, bf16[2048,2560]{1,0:T(8,128)(2,1)} %convolution_convert_fusion.1), kind=kLoop, calls=%fused_computation.10 | loop fusion | flops 62914560 | bytes 62914560
  445.3 21.4 %fusion.45 = (f32[2048]{0:T(1024)S(1)}, bf16[2048,896]{0,1:T(8,128)(2,1)}) fusion(bf16[1,2048,896]{1,2,0:T(8,128)(2,1)S(1)} %copy-done.9, bf16[2048,896]{0,1:T(8,128)(2,1)} %fusion.49, bf16[1,896,2560]{2,0,1:T(2,128)(2,1)} %all-gather.40.cloned.1.call-done, bf16[2048,2560]{1,0:T(8,128)(2,1)} %convolution_convert_fusion.1, f32[2048,2560]{1,0:T(8,128)} %fusion.51), kind=kOutput, calls=%fused_computation.62 | convolution fusion | flops 9437706240 | bytes 47063040 | tf_op jit(solution)/vmap(transpose(jvp()))/dot_general | solution.py:21
  473.6 16.0 %fusion.68 = f32[896,2560]{0,1:T(8,128)} fusion(bf16[2048,2560]{1,0:T(8,128)(2,1)} %fusion.28, bf16[1,2048,896]{1,2,0:T(8,128)(2,1)S(1)} %fusion.67), kind=kOutput, calls=%fused_computation.85 | convolution fusion | flops 9395240960 | bytes 23330816 | tf_op jit(solution)/vmap(transpose(jvp()))/dot_general | solution.py:9
  489.8 16.9 %convolution_convert_fusion = bf16[2048,2560]{1,0:T(8,128)(2,1)} fusion(bf16[1,2560,896]{2,1,0:T(8,128)(2,1)} %all-gather.34.cloned.1.call-done, bf16[1,2048,896]{1,2,0:T(8,128)(2,1)} %copy-done.3), kind=kOutput, calls=%fused_computation.42 | convolution fusion | flops 9400483840 | bytes 18743296 | tf_op jit(solution)/vmap(transpose(jvp()))/dot_general | solution.py:9
  506.6 19.1 %fusion.20 = f32[2560,896]{0,1:T(8,128)} fusion(bf16[2048,2560]{1,0:T(8,128)(2,1)} %convolution_convert_fusion, f32[2048,2560]{1,0:T(8,128)} %fusion.58, bf16[1,2048,896]{1,2,0:T(8,128)(2,1)} %copy.17, f32[2048]{0:T(1024)S(1)} %bitcast.271), kind=kOutput, calls=%fused_computation.30 | convolution fusion | flops 9432203264 | bytes 44310528 | tf_op jit(solution)/vmap(transpose(jvp()))/dot_general | solution.py:21
  525.7 104.9 %fusion.3 = f32[2560,32]{0,1:T(8,128)S(1)} fusion(f32[2560,896]{0,1:T(8,128)} %fusion.20), kind=kCustom, calls=%all-reduce-scatter.3 | all-reduce-scatter fusion | flops 2621441 | bytes 9502720
  652.3 20.6 %fusion.11 = bf16[2048,2560]{1,0:T(8,128)(2,1)} fusion(f32[2048,2560]{1,0:T(8,128)} %fusion.58, f32[2048,2560]{1,0:T(8,128)} %fusion.54, bf16[2048,2560]{1,0:T(8,128)(2,1)S(1)} %bitcast.262), kind=kLoop, calls=%fused_computation.13 | loop fusion | flops 62914560 | bytes 62914560
  687.7 22.4 %fusion.30 = f32[2560,896]{1,0:T(8,128)} fusion(f32[2048,2560]{1,0:T(8,128)} %fusion.46, f32[2048,2560]{1,0:T(8,128)} %fusion.51, bf16[1,2048,896]{2,1,0:T(8,128)(2,1)} %param), kind=kOutput, calls=%fused_computation.46 | convolution fusion | flops 9426698240 | bytes 54788096 | tf_op jit(solution)/vmap(transpose(jvp()))/dot_general | solution.py:9
  725.3 19.3 %fusion.42 = (f32[2048]{0:T(1024)S(1)}, bf16[2048,896]{0,1:T(8,128)(2,1)}) fusion(bf16[1,2048,896]{1,2,0:T(8,128)(2,1)S(1)} %copy-done.1, bf16[2048,896]{0,1:T(8,128)(2,1)S(1)} %fusion.56, bf16[1,896,2560]{2,0,1:T(2,128)(2,1)} %all-gather.32.cloned.1.call-done, bf16[2048,2560]{1,0:T(8,128)(2,1)} %convolution_convert_fusion, f32[2048,2560]{1,0:T(8,128)} %fusion.58), kind=kOutput, calls=%fused_computation.59 | convolution fusion | flops 9437706240 | bytes 47063040 | tf_op jit(solution)/vmap(transpose(jvp()))/dot_general | solution.py:21
  744.6 105.7 %fusion = f32[2560,32]{0,1:T(8,128)S(1)} fusion(f32[2560,896]{0,1:T(8,128)} %fusion.89), kind=kCustom, calls=%all-reduce-scatter | all-reduce-scatter fusion | flops 2621441 | bytes 9502720
  850.4 91.4 %fusion.1 = f32[2560,32]{0,1:T(8,128)S(1)} fusion(f32[2560,896]{0,1:T(8,128)} %fusion.84), kind=kCustom, calls=%all-reduce-scatter.1 | all-reduce-scatter fusion | flops 2621441 | bytes 9502720
  (141 shorter events, 189.2 us)
Async XLA Ops:
  7.2 56.4 %all-gather.30.cloned.1.call-start = ((), (), s32[]{:S(2)}) async-start(), calls=%async_computation.2 | async-start | bytes 9461760 | tf_op jit(solution)/vmap(jvp())/squeeze | solution.py:27
  9.7 105.4 %all-gather.32.cloned.1.call-start = ((), (), s32[]{:S(2)}) async-start(), calls=%async_computation.3 | async-start | bytes 9461760 | tf_op jit(solution)/vmap(jvp())/squeeze | solution.py:27
  12.2 146.0 %all-gather.34.cloned.1.call-start = ((), (), s32[]{:S(2)}) async-start(), calls=%async_computation.4 | async-start | bytes 4730880 | tf_op jit(solution)/vmap(jvp())/squeeze | solution.py:27
  14.0 186.9 %all-gather.38.cloned.1.call-start = ((), (), s32[]{:S(2)}) async-start(), calls=%async_computation.6 | async-start | bytes 4730880 | tf_op jit(solution)/vmap(jvp())/squeeze | solution.py:27
  14.6 237.4 %all-gather.36.cloned.1.call-start = ((), (), s32[]{:S(2)}) async-start(), calls=%async_computation.5 | async-start | bytes 9461760 | tf_op jit(solution)/vmap(jvp())/squeeze | solution.py:27
  15.3 374.3 %all-gather.40.cloned.1.call-start = ((), (), s32[]{:S(2)}) async-start(), calls=%async_computation.7 | async-start | bytes 9461760 | tf_op jit(solution)/vmap(jvp())/squeeze | solution.py:27
  15.9 998.4 %reduce-scatter.21.cloned.1.call-start = ((), (), s32[]{:S(2)}) async-start(), calls=%async_computation.9 | async-start | bytes 9461760
  383.5 559.7 %collective-permute-start.10 = (bf16[2560,32]{0,1:T(8,128)(2,1)}, bf16[2560,32]{0,1:T(8,128)(2,1)}, u32[]{:S(2)}, u32[]{:S(2)}) collective-permute-start(bf16[2560,32]{0,1:T(8,128)(2,1)} %convert.74), channel_id=1, source_target_pairs={{0,3},{1,4},{2,5},{3,6},{4,7},{5,8},{6,9},{7,10},{8,11},{9,12},{10... | collective-permute-start | bytes 491528
  385.6 558.9 %collective-permute-start.8 = (bf16[2560,32]{0,1:T(8,128)(2,1)}, bf16[2560,32]{0,1:T(8,128)(2,1)}, u32[]{:S(2)}, u32[]{:S(2)}) collective-permute-start(bf16[2560,32]{0,1:T(8,128)(2,1)} %convert.74), channel_id=1, source_target_pairs={{0,1},{1,2},{2,3},{3,4},{4,5},{5,6},{6,7},{7,8},{8,9},{9,10},{10,1... | collective-permute-start | bytes 491528
  387.6 576.2 %collective-permute-start.9 = (bf16[2560,32]{0,1:T(8,128)(2,1)}, bf16[2560,32]{0,1:T(8,128)(2,1)}, u32[]{:S(2)}, u32[]{:S(2)}) collective-permute-start(bf16[2560,32]{0,1:T(8,128)(2,1)} %convert.74), channel_id=1, source_target_pairs={{0,2},{1,3},{2,4},{3,5},{4,6},{5,7},{6,8},{7,9},{8,10},{9,11},{10,... | collective-permute-start | bytes 491528
  489.7 525.6 %reduce-scatter.19.cloned.1.call-start = ((), (), s32[]{:S(2)}) async-start(), calls=%async_computation.8 | async-start | bytes 9461760
  632.1 309.8 %collective-permute-start.11 = (bf16[2560,28]{0,1:T(8,128)(2,1)}, bf16[2560,28]{0,1:T(8,128)(2,1)}, u32[]{:S(2)}, u32[]{:S(2)}) collective-permute-start(bf16[2560,28]{0,1:T(8,128)(2,1)} %slice.26), channel_id=1, source_target_pairs={{0,4},{1,5},{2,6},{3,7},{4,8},{5,9},{6,10},{7,11},{8,12},{9,13},{1... | collective-permute-start | bytes 430088
  634.3 339.5 %collective-permute-start.12 = (bf16[2560,32]{0,1:T(8,128)(2,1)}, bf16[2560,32]{0,1:T(8,128)(2,1)}, u32[]{:S(2)}, u32[]{:S(2)}) collective-permute-start(bf16[2560,32]{0,1:T(8,128)(2,1)} %convert.75), channel_id=1, source_target_pairs={{0,1},{1,2},{2,3},{3,4},{4,5},{5,6},{6,7},{7,8},{8,9},{9,10},{10,1... | collective-permute-start | bytes 491528
  941.9 34.0 %collective-permute-start.13 = (bf16[2560,32]{0,1:T(8,128)(2,1)}, bf16[2560,32]{0,1:T(8,128)(2,1)S(1)}, u32[]{:S(2)}, u32[]{:S(2)}) collective-permute-start(bf16[2560,32]{0,1:T(8,128)(2,1)} %convert.75), channel_id=1, source_target_pairs={{0,2},{1,3},{2,4},{3,5},{4,6},{5,7},{6,8},{7,9},{8,10},{9,11},{10,... | collective-permute-start | bytes 491528
  943.2 34.0 %collective-permute-start.14 = (bf16[2560,32]{0,1:T(8,128)(2,1)}, bf16[2560,32]{0,1:T(8,128)(2,1)S(1)}, u32[]{:S(2)}, u32[]{:S(2)}) collective-permute-start(bf16[2560,32]{0,1:T(8,128)(2,1)} %convert.75), channel_id=1, source_target_pairs={{0,3},{1,4},{2,5},{3,6},{4,7},{5,8},{6,9},{7,10},{8,11},{9,12},{10... | collective-permute-start | bytes 491528
  944.6 28.0 %collective-permute-start.15 = (bf16[2560,28]{0,1:T(8,128)(2,1)S(1)}, bf16[2560,28]{0,1:T(8,128)(2,1)S(1)}, u32[]{:S(2)}, u32[]{:S(2)}) collective-permute-start(bf16[2560,28]{0,1:T(8,128)(2,1)S(1)} %copy-done.13), channel_id=1, source_target_pairs={{0,4},{1,5},{2,6},{3,7},{4,8},{5,9},{6,10},{7,11},{8,12},{9,13},{1... | collective-permute-start | bytes 430088
  963.8 20.5 %collective-permute-start = (bf16[2560,32]{0,1:T(8,128)(2,1)}, bf16[2560,32]{0,1:T(8,128)(2,1)S(1)}, u32[]{:S(2)}, u32[]{:S(2)}) collective-permute-start(bf16[2560,32]{0,1:T(8,128)(2,1)} %convert.76), channel_id=1, source_target_pairs={{0,1},{1,2},{2,3},{3,4},{4,5},{5,6},{6,7},{7,8},{8,9},{9,10},{10,1... | collective-permute-start | bytes 491528
  972.5 22.5 %collective-permute-start.1 = (bf16[2560,32]{0,1:T(8,128)(2,1)}, bf16[2560,32]{0,1:T(8,128)(2,1)S(1)}, u32[]{:S(2)}, u32[]{:S(2)}) collective-permute-start(bf16[2560,32]{0,1:T(8,128)(2,1)} %convert.76), channel_id=1, source_target_pairs={{0,2},{1,3},{2,4},{3,5},{4,6},{5,7},{6,8},{7,9},{8,10},{9,11},{10,... | collective-permute-start | bytes 491528
  973.9 31.2 %collective-permute-start.2 = (bf16[2560,32]{0,1:T(8,128)(2,1)}, bf16[2560,32]{0,1:T(8,128)(2,1)}, u32[]{:S(2)}, u32[]{:S(2)}) collective-permute-start(bf16[2560,32]{0,1:T(8,128)(2,1)} %convert.76), channel_id=1, source_target_pairs={{0,3},{1,4},{2,5},{3,6},{4,7},{5,8},{6,9},{7,10},{8,11},{9,12},{10... | collective-permute-start | bytes 491528
  975.9 7.1 collective-permute-start.3
  977.2 33.1 %collective-permute-start.4 = (bf16[2560,32]{0,1:T(8,128)(2,1)}, bf16[2560,32]{0,1:T(8,128)(2,1)}, u32[]{:S(2)}, u32[]{:S(2)}) collective-permute-start(bf16[2560,32]{0,1:T(8,128)(2,1)} %convert.77), channel_id=1, source_target_pairs={{0,1},{1,2},{2,3},{3,4},{4,5},{5,6},{6,7},{7,8},{8,9},{9,10},{10,1... | collective-permute-start | bytes 491528
  983.0 27.3 %collective-permute-start.5 = (bf16[2560,32]{0,1:T(8,128)(2,1)}, bf16[2560,32]{0,1:T(8,128)(2,1)S(1)}, u32[]{:S(2)}, u32[]{:S(2)}) collective-permute-start(bf16[2560,32]{0,1:T(8,128)(2,1)} %convert.77), channel_id=1, source_target_pairs={{0,2},{1,3},{2,4},{3,5},{4,6},{5,7},{6,8},{7,9},{8,10},{9,11},{10,... | collective-permute-start | bytes 491528
  984.3 25.9 %collective-permute-start.6 = (bf16[2560,32]{0,1:T(8,128)(2,1)}, bf16[2560,32]{0,1:T(8,128)(2,1)S(1)}, u32[]{:S(2)}, u32[]{:S(2)}) collective-permute-start(bf16[2560,32]{0,1:T(8,128)(2,1)} %convert.77), channel_id=1, source_target_pairs={{0,3},{1,4},{2,5},{3,6},{4,7},{5,8},{6,9},{7,10},{8,11},{9,12},{10... | collective-permute-start | bytes 491528
  995.7 14.5 %collective-permute-start.7 = (bf16[2560,28]{0,1:T(8,128)(2,1)}, bf16[2560,28]{0,1:T(8,128)(2,1)S(1)}, u32[]{:S(2)}, u32[]{:S(2)}) collective-permute-start(bf16[2560,28]{0,1:T(8,128)(2,1)} %slice.25), channel_id=1, source_target_pairs={{0,4},{1,5},{2,6},{3,7},{4,8},{5,9},{6,10},{7,11},{8,12},{9,13},{1... | collective-permute-start | bytes 430088
  (23 other events, 783.9 us)
Sparse Core Ops, SparseCore 0:
  10.1 53.4 all-gather.29
  66.3 48.7 all-gather.31
  117.2 40.9 all-gather.33
  160.2 40.7 all-gather.37
  203.4 48.5 all-gather.35
  254.5 49.5 all-gather.39
  489.8 102.8 reduce-scatter.20
  710.2 102.7 reduce-scatter.18
where the time goes:
time: 1030 us; the launch traced here: 1020 us
  blocking collectives  394 us (38%)
  matrix products  304 us (30%)
  waiting for transfers between devices  131 us (13%)
  other arithmetic  80.8 us (8%)
  local copies, waits for them, and re-layouts  55.8 us (5%)
  starting transfers between devices  43.5 us (4%)
  between operations  15.2 us (1%)
    unnamed x4, blocking collectives  394 us
    squeeze x6, waiting for transfers between devices, stack(): h = layer(h, {name: w[number] for name, w in weights.items()})  129 us
    dot_general x6, matrix products, layer(): up = jnp.dot(a, w['w_up'], preferred_element_type=jnp.float32)  117 us
    dot_general x6, matrix products, layer(): gate = jnp.dot(a, w['w_gate'], preferred_element_type=jnp.float32)  98.9 us
    dot_general x5, matrix products, matmul(): jnp.dot(a, w, preferred_element_type=jnp.float32).astype(jnp.bfloat16)  88.1 us
    unnamed x8, other arithmetic  60.9 us
    unnamed x59, local copies, waits for them, and re-layouts  49.1 us
    unnamed x18, starting transfers between devices  43.2 us
  transfers between devices with their start and end apart: 24, of which 5 were waited for; matrix products, arithmetic and copies ran while one was open for 80% of the time, Pallas kernels for 0%

commit v1 on v0

v1 whole, which is shorter than its diff:
```python
import functools
import math

import jax
import jax.numpy as jnp
from jax import lax
from jax.experimental import pallas as pl
from jax.experimental.pallas import tpu as pltpu
from jax.sharding import PartitionSpec as P

MESH = pl.DeviceIdType.MESH
F32, BF16 = jnp.float32, jnp.bfloat16


class Place:
    def __init__(self, side):
        me = lax.axis_index("dp")
        self.side = side
        self.core = me % 2
        chip = me // 2
        self.x, self.y = chip // side, chip % side
        first = self.core == 0
        self.a = jnp.where(first, self.x, self.y)
        self.b = jnp.where(first, self.y, self.x)

    def chip(self, a, b, core=None):
        first = (self.core if core is None else core) == 0
        return jnp.where(first, a * self.side + b, b * self.side + a)

    def step(self, v, by):
        return (v + by + self.side) % self.side

    def at(self, a, b):
        return {"dp": self.chip(a, b) * 2 + self.core}

    def a_next(self, by):
        return self.at(self.step(self.a, by), self.b)

    def b_next(self, by):
        return self.at(self.a, self.step(self.b, by))

    def partner(self):
        return {"dp": self.chip(self.a, self.b) * 2 + 1 - self.core}


def greet(place):
    barrier = pltpu.get_barrier_semaphore()
    peers = [place.a_next(1), place.a_next(-1), place.b_next(1), place.b_next(-1), place.partner()]
    for peer in peers:
        pl.semaphore_signal(barrier, inc=1, device_id=peer, device_id_type=MESH)
    pl.semaphore_wait(barrier, len(peers))


def halves(width):
    first = -(-width // 256) * 128
    return ((0, first), (first, width - first))


def part(place, split, ref, chip, core, half=None):
    rows, columns = ref.shape[1:]
    start, width, row, height = 0, columns, 0, rows
    if split == "columns":
        width = columns // 2
        start = core * width
    else:
        height = rows // 2
        row = pl.multiple_of(core * height, 16)
    if half is not None:
        offset, size = halves(width)[half]
        start, width = start + offset, size
    if not isinstance(start, int):
        start = pl.multiple_of(start, 128)
    return ref.at[chip, pl.ds(row, height), pl.ds(start, width)]


def block_shape(split, rows, columns):
    return (rows, columns // 2) if split == "columns" else (rows // 2, columns)


def remote(src, dst, send, recv, peer):
    copy = pltpu.make_async_remote_copy(
        src_ref=src, dst_ref=dst, send_sem=send, recv_sem=recv, device_id=peer, device_id_type=MESH
    )
    return copy


class Gather:
    COPIES = 36

    def __init__(self, place, split, own, full, send, recv):
        self.place, self.split, self.own, self.full, self.send, self.recv = place, split, own, full, send, recv

    def copy(self, slot, a, b, peer, half=None, mine=False):
        p = self.place
        chip = p.chip(a, b)
        dst = part(p, self.split, self.full, chip, p.core, half)
        src = part(p, self.split, self.own, 0, p.core, half) if mine else dst
        return remote(src, dst, self.send.at[slot], self.recv.at[slot], peer)

    def spread(self, k, a, mine=False):
        p = self.place
        base = 4 + 4 * k
        self.copy(base, a, p.b, p.b_next(1), mine=mine).start()
        self.copy(base + 1, a, p.b, p.b_next(-1), mine=mine).start()
        self.copy(20 + 4 * k, a, p.b, p.partner(), mine=mine).start()

    def keep(self, stage, sem):
        p = self.place
        into = pltpu.make_async_copy(part(p, self.split, self.own, 0, p.core), stage, sem)
        onto = pltpu.make_async_copy(stage, part(p, self.split, self.full, p.chip(p.a, p.b), p.core), sem)
        return into, onto

    def keep_in(self, stage, sem):
        self.keep(stage, sem)[0].start()

    def keep_out(self, stage, sem):
        into, onto = self.keep(stage, sem)
        into.wait()
        onto.start()

    def kept(self, stage, sem):
        self.keep(stage, sem)[1].wait()

    def first(self):
        p = self.place
        self.copy(0, p.a, p.b, p.a_next(1), mine=True).start()
        self.copy(1, p.a, p.b, p.a_next(-1), mine=True).start()
        self.spread(0, p.a, mine=True)

    def second(self):
        p = self.place
        left, right = p.step(p.a, -1), p.step(p.a, 1)
        self.copy(0, left, p.b, p.a_next(1)).wait_recv()
        self.copy(2, left, p.b, p.a_next(1), half=0).start()
        self.copy(1, right, p.b, p.a_next(1)).wait_recv()
        self.copy(3, right, p.b, p.a_next(-1), half=1).start()
        self.spread(1, left)
        self.spread(2, right)

    def third(self):
        p = self.place
        far = p.step(p.a, 2)
        self.copy(2, far, p.b, p.a_next(1), half=0).wait_recv()
        self.copy(3, far, p.b, p.a_next(1), half=1).wait_recv()
        self.spread(3, far)

    def rows(self):
        p = self.place
        return (p.a, p.step(p.a, -1), p.step(p.a, 1), p.step(p.a, 2))

    def relay(self, k):
        p = self.place
        a = self.rows()[k]
        base = 4 + 4 * k
        left, right = p.step(p.b, -1), p.step(p.b, 1)
        self.copy(base, a, left, p.b_next(1)).wait_recv()
        self.copy(base + 2, a, left, p.b_next(1), half=0).start()
        self.copy(base + 1, a, right, p.b_next(1)).wait_recv()
        self.copy(base + 3, a, right, p.b_next(-1), half=1).start()
        self.copy(20 + 4 * k + 1, a, left, p.partner()).start()
        self.copy(20 + 4 * k + 2, a, right, p.partner()).start()

    def last(self, k):
        p = self.place
        a = self.rows()[k]
        base = 4 + 4 * k
        far = p.step(p.b, 2)
        self.copy(base + 2, a, far, p.b_next(1), half=0).wait_recv()
        self.copy(base + 3, a, far, p.b_next(1), half=1).wait_recv()
        self.copy(20 + 4 * k + 3, a, far, p.partner()).start()

    def finish(self):
        p = self.place
        def wait_send(slot, like):
            remote(like, like, self.send.at[slot], self.recv.at[slot], p.a_next(1)).wait_send()

        block = part(p, self.split, self.full, 0, p.core)
        half = [part(p, self.split, self.full, 0, p.core, h) for h in (0, 1)]
        theirs = part(p, self.split, self.full, 0, 1 - p.core)
        for base in (0, 4, 8, 12, 16):
            wait_send(base, block)
            wait_send(base + 1, block)
            wait_send(base + 2, half[0])
            wait_send(base + 3, half[1])
        for slot in range(20, 36):
            wait_send(slot, block)
            remote(theirs, theirs, self.send.at[slot], self.recv.at[slot], p.partner()).wait_recv()

    def steps(self):
        return (
            [self.first, self.second, self.third]
            + [functools.partial(self.relay, k) for k in range(4)]
            + [functools.partial(self.last, k) for k in range(4)]
            + [self.finish]
        )


def woven(lists, lag):
    out = []
    longest = max(len(l) for l in lists)
    for t in range(longest + lag * (len(lists) - 1)):
        for i, l in enumerate(lists):
            if 0 <= t - lag * i < len(l):
                out.append(l[t - lag * i])
    return out


def gather_kernel(side, splits, *refs):
    n = len(splits)
    own, full, (stage, send, recv, local) = refs[:n], refs[n : 2 * n], (refs[2 * n : 3 * n], *refs[3 * n :])
    place = Place(side)
    greet(place)
    gathers = [Gather(place, s, o, f, send.at[i], recv.at[i]) for i, (s, o, f) in enumerate(zip(splits, own, full))]
    steps = [functools.partial(g.keep_in, stage[i], local.at[i]) for i, g in enumerate(gathers)]
    woven_steps = woven([g.steps() for g in gathers], 1)
    steps += woven_steps[: 2 * n]
    steps += [functools.partial(g.keep_out, stage[i], local.at[i]) for i, g in enumerate(gathers)]
    steps += woven_steps[2 * n :]
    steps += [functools.partial(g.kept, stage[i], local.at[i]) for i, g in enumerate(gathers)]
    for step in steps:
        step()


def gather(side, chips, splits, blocks, collective_id):
    n = len(splits)
    return pl.pallas_call(
        functools.partial(gather_kernel, side, splits),
        out_shape=[jax.ShapeDtypeStruct((chips, *b.shape[1:]), b.dtype) for b in blocks],
        in_specs=[pl.BlockSpec(memory_space=pl.ANY)] * n,
        out_specs=[pl.BlockSpec(memory_space=pl.ANY)] * n,
        scratch_shapes=[pltpu.VMEM(block_shape(s, *b.shape[1:]), b.dtype) for s, b in zip(splits, blocks)]
        + [
            pltpu.SemaphoreType.DMA((n, Gather.COPIES)),
            pltpu.SemaphoreType.DMA((n, Gather.COPIES)),
            pltpu.SemaphoreType.DMA((n,)),
        ],
        compiler_params=pltpu.CompilerParams(collective_id=collective_id, has_side_effects=True),
        name="gather",
    )(*blocks)


class Scatter:
    SEMS = 48

    @staticmethod
    def scratch(side, split, rows, columns):
        h, w = block_shape(split, rows, columns)
        (_, w0), (_, w1) = halves(w)
        n = side
        return [
            pltpu.VMEM((n, n, h, w), BF16),
            pltpu.VMEM((n, n, h, w), BF16),
            pltpu.VMEM((n, h, w0), BF16),
            pltpu.VMEM((n, h, w1), BF16),
            pltpu.VMEM((2, n, h, w), BF16),
            pltpu.VMEM((h, w0), BF16),
            pltpu.VMEM((h, w1), BF16),
            pltpu.VMEM((2, h, w), BF16),
        ]

    def __init__(self, place, split, terms, out, bufs, send, recv):
        self.place, self.split, self.terms, self.out, self.send, self.recv = place, split, terms, out, send, recv
        self.sums, self.theirs, self.h0, self.h1, self.full, self.g0, self.g1, self.last_in = bufs
        self.w = self.sums.shape[-1]
        (_, self.w0), (_, self.w1) = halves(self.w)

    def copies(self):
        p, n = self.place, self.place.side
        other = 1 - p.core
        for b in range(n):
            for a in range(n):
                slot = b * n + a
                mine = pltpu.make_async_copy(
                    part(p, self.split, self.terms, p.chip(a, b), p.core), self.sums.at[b, a], self.send.at[16 + slot]
                )
                sent = remote(
                    part(p, self.split, self.terms, p.chip(a, b, other), other),
                    self.theirs.at[b, a],
                    self.send.at[slot],
                    self.recv.at[slot],
                    p.partner(),
                )
                yield b, a, mine, sent

    def start(self):
        for _, _, mine, sent in self.copies():
            sent.start()
            mine.start()

    def pair(self, k):
        p = self.place
        b = p.step(p.b, k)
        for a in range(p.side):
            slot = b * p.side + a
            pltpu.make_async_copy(
                self.sums.at[b, a], self.sums.at[b, a], self.send.at[16 + slot]
            ).wait()
            remote(
                self.sums.at[b, a], self.theirs.at[b, a], self.send.at[slot], self.recv.at[slot], p.partner()
            ).wait()
            self.sums[b, a] = (self.sums[b, a].astype(F32) + self.theirs[b, a].astype(F32)).astype(BF16)

    def ring_b(self, slot, b, src, dst, by):
        return remote(src, dst, self.send.at[32 + slot], self.recv.at[32 + slot], self.place.b_next(by))

    def ring_a(self, slot, src, dst, by):
        return remote(src, dst, self.send.at[36 + slot], self.recv.at[36 + slot], self.place.a_next(by))

    def b_copies(self):
        p = self.place
        far, right, left = p.step(p.b, 2), p.step(p.b, 1), p.step(p.b, -1)
        lo, hi = pl.ds(0, self.w0), pl.ds(self.w0, self.w1)
        every = pl.ds(0, p.side)
        rows = pl.ds(0, self.sums.shape[2])
        return (
            self.ring_b(0, far, self.sums.at[far, every, rows, lo], self.h0, 1),
            self.ring_b(1, far, self.sums.at[far, every, rows, hi], self.h1, -1),
            self.ring_b(2, right, self.sums.at[right], self.full.at[0], 1),
            self.ring_b(3, left, self.sums.at[left], self.full.at[1], -1),
        )

    def b_out(self):
        c = self.b_copies()
        c[0].start()
        c[1].start()

    def b_relay(self):
        p, n = self.place, self.place.side
        c = self.b_copies()
        c[0].wait_recv()
        right, left = p.step(p.b, 1), p.step(p.b, -1)
        for a in range(n):
            self.sums[right, a, :, : self.w0] = (
                self.sums[right, a, :, : self.w0].astype(F32) + self.h0[a].astype(F32)
            ).astype(BF16)
        c[2].start()
        c[1].wait_recv()
        for a in range(n):
            self.sums[left, a, :, self.w0 :] = (
                self.sums[left, a, :, self.w0 :].astype(F32) + self.h1[a].astype(F32)
            ).astype(BF16)
        c[3].start()

    def a_copies(self):
        p = self.place
        far, right, left = p.step(p.a, 2), p.step(p.a, 1), p.step(p.a, -1)
        lo, hi = pl.ds(0, self.w0), pl.ds(self.w0, self.w1)
        rows = pl.ds(0, self.sums.shape[2])
        s = self.theirs
        return (
            self.ring_a(0, s.at[0, far, rows, lo], self.g0, 1),
            self.ring_a(1, s.at[0, far, rows, hi], self.g1, -1),
            self.ring_a(2, s.at[0, right], self.last_in.at[0], 1),
            self.ring_a(3, s.at[0, left], self.last_in.at[1], -1),
        )

    def b_in(self):
        p, n = self.place, self.place.side
        c = self.b_copies()
        c[2].wait_recv()
        c[3].wait_recv()
        for a in range(n):
            self.theirs[0, a] = (
                self.sums[p.b, a].astype(F32) + self.full[0, a].astype(F32) + self.full[1, a].astype(F32)
            ).astype(BF16)
        c = self.a_copies()
        c[0].start()
        c[1].start()

    def a_relay(self):
        p = self.place
        c = self.a_copies()
        right, left = p.step(p.a, 1), p.step(p.a, -1)
        c[0].wait_recv()
        self.theirs[0, right, :, : self.w0] = (
            self.theirs[0, right, :, : self.w0].astype(F32) + self.g0[...].astype(F32)
        ).astype(BF16)
        c[2].start()
        c[1].wait_recv()
        self.theirs[0, left, :, self.w0 :] = (
            self.theirs[0, left, :, self.w0 :].astype(F32) + self.g1[...].astype(F32)
        ).astype(BF16)
        c[3].start()

    def finish(self):
        p = self.place
        c = self.a_copies()
        c[2].wait_recv()
        c[3].wait_recv()
        self.out[...] = (
            self.theirs[0, p.a].astype(F32) + self.last_in[0].astype(F32) + self.last_in[1].astype(F32)
        ).astype(BF16)
        for copy in (*self.b_copies(), *c):
            copy.wait_send()

    def steps(self):
        return [
            self.start,
            functools.partial(self.pair, 2),
            self.b_out,
            functools.partial(self.pair, 1),
            functools.partial(self.pair, -1),
            functools.partial(self.pair, 0),
            self.b_relay,
            self.b_in,
            self.a_relay,
            self.finish,
        ]


def scatter_kernel(side, splits, *refs):
    n = len(splits)
    terms, outs, bufs, (send, recv) = refs[:n], refs[n : 2 * n], refs[2 * n : 10 * n], refs[10 * n :]
    place = Place(side)
    greet(place)
    scatters = [
        Scatter(place, splits[i], terms[i], outs[i], bufs[8 * i : 8 * i + 8], send.at[i], recv.at[i]) for i in range(n)
    ]
    lists = [s.steps() for s in scatters]
    for l in lists:
        l.pop(0)()
    for step in woven(lists, 2):
        step()


def scatter(side, splits, terms, collective_id):
    n = len(splits)
    shapes = [block_shape(s, *t.shape[1:]) for s, t in zip(splits, terms)]
    return pl.pallas_call(
        functools.partial(scatter_kernel, side, splits),
        out_shape=[jax.ShapeDtypeStruct(s, BF16) for s in shapes],
        in_specs=[pl.BlockSpec(memory_space=pl.ANY)] * n,
        out_specs=[pl.BlockSpec(memory_space=pltpu.VMEM)] * n,
        scratch_shapes=[b for s, t in zip(splits, terms) for b in Scatter.scratch(side, s, *t.shape[1:])]
        + [pltpu.SemaphoreType.DMA((n, Scatter.SEMS)), pltpu.SemaphoreType.DMA((n, Scatter.SEMS))],
        compiler_params=pltpu.CompilerParams(
            collective_id=collective_id, has_side_effects=True, vmem_limit_bytes=56 * 2**20
        ),
        name="scatter",
    )(*terms)


def dot(a, w, dims=((1,), (0,))):
    return lax.dot_general(a, w, (dims, ((), ())), preferred_element_type=F32)


def normed(h):
    wide = h.astype(F32)
    scale = lax.rsqrt(jnp.mean(wide**2, -1, keepdims=True) + 1e-6)
    return (wide * scale).astype(BF16), scale


def norm_back(h, scale, da):
    wide, ct = h.astype(F32), da.astype(F32)
    inner = jnp.sum(ct * wide, -1, keepdims=True)
    return (ct * scale - wide * (scale**3) * inner / h.shape[-1]).astype(BF16)


def solution(mesh):
    n = mesh.shape["dp"]
    chips = n // 2
    side = math.isqrt(chips)
    splits = ("columns", "columns", "rows")
    swap = [(i, i ^ 1) for i in range(n)]

    def step(x, dy, w_gate, w_up, w_down):
        x, dy = x[0], dy[0]
        layers, d_own, ff = w_gate.shape
        f_own, d = w_down.shape[1:]
        core = lax.axis_index("dp") % 2

        both = jnp.stack([w_gate, w_up])
        other = lax.ppermute(both, "dp", swap)
        both = jnp.where(core == 0, jnp.concatenate([both, other], 2), jnp.concatenate([other, both], 2))
        downs = jnp.pad(w_down, ((0, 0), (0, f_own), (0, 0)))
        downs = jnp.where(core == 0, downs, jnp.roll(downs, f_own, 1))
        weights = []
        for l in range(layers):
            full = gather(side, chips, splits, [both[0, l : l + 1], both[1, l : l + 1], downs[l : l + 1]], 1)
            weights.append([f.reshape(-1, f.shape[-1]) for f in full])

        def forward(h, w):
            a, scale = normed(h)
            gate, up = dot(a, w[0]), dot(a, w[1])
            return a, scale, gate, up, (jax.nn.silu(gate) * up).astype(BF16)

        def backward(h, saved, w, g):
            a, scale, gate, up, p = saved
            dp = dot(g, w[2], ((1,), (1,))).astype(BF16).astype(F32)
            sig = jax.nn.sigmoid(gate)
            d_up = (dp * (gate * sig)).astype(BF16)
            d_gate = (dp * up * (sig * (1 + gate * (1 - sig)))).astype(BF16)
            down = dot(p, g, ((0,), (0,))).astype(BF16)
            by_gate = dot(a, d_gate, ((0,), (0,))).astype(BF16)
            by_up = dot(a, d_up, ((0,), (0,))).astype(BF16)
            da = (
                dot(d_gate, w[0], ((1,), (1,))).astype(BF16).astype(F32)
                + dot(d_up, w[1], ((1,), (1,))).astype(BF16).astype(F32)
            ).astype(BF16)
            dh = (g.astype(F32) + norm_back(h, scale, da).astype(F32)).astype(BF16)
            terms = [t.reshape(chips, -1, t.shape[-1]) for t in (by_gate, by_up, down)]
            return dh, scatter(side, splits, terms, 2)

        hs, saved = [x], []
        for l in range(layers):
            saved.append(forward(hs[l], weights[l]))
            hs.append((hs[l].astype(F32) + dot(saved[l][4], weights[l][2]).astype(BF16).astype(F32)).astype(BF16))
        g, sums = dy, [None] * layers
        for l in reversed(range(layers)):
            g, sums[l] = backward(hs[l], saved[l], weights[l], g)
        mine = jnp.stack([jnp.stack([s[0], s[1]]) for s in sums], 1)
        lower, upper = mine[:, :, :d_own], mine[:, :, d_own:]
        got = lax.ppermute(jnp.where(core == 0, upper, lower), "dp", swap)
        by = jnp.where(core == 0, jnp.concatenate([lower, got], -1), jnp.concatenate([got, upper], -1))
        return g[None], by[0], by[1], jnp.stack([s[2] for s in sums])

    wspec = P(None, "dp", None)
    out = P("rep", "dp", None)
    rows = P(("rep", "dp"), None, None)
    return jax.shard_map(
        step, mesh=mesh, in_specs=(rows, rows, wspec, wspec, wspec), out_specs=(rows, out, out, out), check_vma=False
    )
```

time: 1030 us -> 570 us (0.55)
  blocking collectives: 394 us -> 0 us
  Pallas kernels: 0 us -> 209 us
  waiting for transfers between devices: 131 us -> 0.01 us
  other arithmetic: 80.8 us -> 15.1 us
  starting transfers between devices: 43.5 us -> 4.62 us
  local copies, waits for them, and re-layouts: 55.8 us -> 24.2 us
  between operations: 15.2 us -> 1.33 us
    unnamed x4 -> x0, blocking collectives: 394 us -> none
    pallas_call x0 -> x4, Pallas kernels: none -> 209 us  [the longest x2 118 us: scatter(): pl.pallas_call(functools.partial(scatter_kernel, side, splits), out_shape...]
    squeeze x6 -> x0, waiting for transfers between devices: 129 us -> none  [stack(): h = layer(h, {name: w[number] for name, w in weights.items()})]
    unnamed x8 -> x2, other arithmetic: 60.9 us -> 0.01 us
    unnamed x18 -> x0, starting transfers between devices: 43.2 us -> none
    unnamed x59 -> x45, local copies, waits for them, and re-layouts: 49.1 us -> 20.4 us
    add_any x2 -> x0, other arithmetic: 14.2 us -> none  [normed(): wide = h.astype(jnp.float32)]
  transfers between devices with their start and end apart: 24 -> 2, of which waited for: 5 -> 0; matrix products, arithmetic and copies ran while one was open for 80% -> 8% of each run, Pallas kernels for 0% -> 0%
where the time goes in v1:
time: 570 us; the launch traced here: 561 us
  matrix products  307 us (54%)
  Pallas kernels  209 us (37%)
  local copies, waits for them, and re-layouts  24.2 us (4%)
  other arithmetic  15.1 us (3%)
    dot_general x17, matrix products, dot(): return lax.dot_general(a, w, (dims, ((), ())), preferred_element_type=F32)  307 us
    pallas_call x2, Pallas kernels, scatter(): pl.pallas_call(functools.partial(scatter_kernel, side, splits), out_shape...  118 us
    pallas_call x2, Pallas kernels, gather(): pl.pallas_call(functools.partial(gather_kernel, side, splits), out_shape=...  91.3 us
    unnamed x45, local copies, waits for them, and re-layouts  20.4 us
  transfers between devices with their start and end apart: 2, of which 0 were waited for; matrix products, arithmetic and copies ran while one was open for 8% of the time, Pallas kernels for 0%

profile of v1, /device:TPU:97, one launch (start us, length us, event | category | flops | bytes accessed | tf_op | source)
XLA Modules:
  0.0 561.4 jit_solution(7727726260959292164)
XLA Ops:
  4.6 6.0 %copy.33 = bf16[1,2048,896]{1,2,0:T(8,128)(2,1)} copy(bf16[1,2048,896]{2,1,0:T(8,128)(2,1)} %param.5) | data formatting | bytes 7340032 | tf_op args[0]
  13.5 6.2 %copy.27 = bf16[1,2048,896]{1,2,0:T(8,128)(2,1)} copy(bf16[1,2048,896]{2,1,0:T(8,128)(2,1)} %param.6) | data formatting | bytes 7340032 | tf_op args[1]
  22.8 46.9 %gather.3 = (bf16[16,56,2560]{2,1,0:T(8,128)(2,1)}, bf16[16,56,2560]{2,1,0:T(8,128)(2,1)}, bf16[16,160,896]{2,1,0:T(8,128)(2,1)}) custom-call(bf16[1,56,2560]{2,1,0:T(8,128)(2,1)} %get-tuple-element.45.refs_0_, bf16[1,56,2560]{2,1,0:T(8,128)(2,1)} %get-tuple-element.44.refs_1_, bf16[1,160,896]{2,1,0:T(8,128)(2,1)} %get-tuple-element.50.refs_2_), custom_call_target="tpu_custom_call" | custom-call | tf_op jit(solution)/shard_map/gather/pallas_call | solution.py:226
  69.8 18.1 %fusion.38 = f32[2048,2560]{0,1:T(8,128)} fusion(bf16[896,2560]{1,0:T(8,128)(2,1)} %bitcast.132, bf16[1,2048,896]{1,2,0:T(8,128)(2,1)} %copy.33, f32[2048]{0:T(1024)S(1)} %get-tuple-element.52), kind=kOutput, calls=%fused_computation.63 | convolution fusion | flops 9400745984 | bytes 29237248 | tf_op jit(solution)/shard_map/dot_general | solution.py:444
  87.9 24.5 %multiply_convert_fusion.1 = (bf16[2048,2560]{0,1:T(8,128)(2,1)}, f32[2048,2560]{0,1:T(8,128)}) fusion(f32[2048,2560]{0,1:T(8,128)} %fusion.38, bf16[896,2560]{1,0:T(8,128)(2,1)} %bitcast.130, bf16[1,2048,896]{1,2,0:T(8,128)(2,1)S(1)} %copy-done, f32[2048]{0:T(1024)S(1)} %get-tuple-element.52), kind=kOutput, calls=%fused_computation.13 | convolution fusion | flops 9432203264 | bytes 60694528 | tf_op jit(solution)/shard_map/dot_general | solution.py:444
  112.4 15.8 %fusion.25 = (f32[2048]{0:T(1024)S(1)}, bf16[2048,896]{0,1:T(8,128)(2,1)}) fusion(bf16[2048,2560]{0,1:T(8,128)(2,1)} %get-tuple-element.55, bf16[2560,896]{1,0:T(8,128)(2,1)} %bitcast.134, bf16[1,2048,896]{1,2,0:T(8,128)(2,1)S(1)} %copy-done), kind=kOutput, calls=%fused_computation.43 | convolution fusion | flops 9409918976 | bytes 22421504 | tf_op jit(solution)/shard_map/dot_general | solution.py:444
  128.8 44.3 %gather.2 = (bf16[16,56,2560]{2,1,0:T(8,128)(2,1)}, bf16[16,56,2560]{2,1,0:T(8,128)(2,1)}, bf16[16,160,896]{2,1,0:T(8,128)(2,1)}) custom-call(bf16[1,56,2560]{2,1,0:T(8,128)(2,1)} %get-tuple-element.46.refs_0_, bf16[1,56,2560]{2,1,0:T(8,128)(2,1)} %get-tuple-element.43.refs_1_, bf16[1,160,896]{2,1,0:T(8,128)(2,1)} %get-tuple-element.49.refs_2_), custom_call_target="tpu_custom_call" | custom-call | tf_op jit(solution)/shard_map/gather/pallas_call | solution.py:226
  173.2 18.9 %fusion.46 = f32[2048,2560]{0,1:T(8,128)} fusion(bf16[896,2560]{1,0:T(8,128)(2,1)} %bitcast.136, bf16[2048,896]{0,1:T(8,128)(2,1)} %get-tuple-element.58, f32[2048]{0:T(1024)S(1)} %get-tuple-element.54), kind=kOutput, calls=%fused_computation.65 | convolution fusion | flops 9400745984 | bytes 29237248 | tf_op jit(solution)/shard_map/dot_general | solution.py:444
  192.1 14.5 %fusion.44 = f32[2048,2560]{0,1:T(8,128)} fusion(bf16[896,2560]{1,0:T(8,128)(2,1)S(1)} %bitcast.141, bf16[2048,896]{0,1:T(8,128)(2,1)S(1)} %copy-done.5, f32[2048]{0:T(1024)S(1)} %get-tuple-element.54), kind=kOutput, calls=%fused_computation.64 | convolution fusion | flops 9400745984 | bytes 29237248 | tf_op jit(solution)/shard_map/dot_general | solution.py:444
  206.6 21.4 %fusion.30 = bf16[2560,896]{1,0:T(8,128)(2,1)} fusion(f32[2048,2560]{0,1:T(8,128)} %fusion.46, bf16[1,2048,896]{2,1,0:T(8,128)(2,1)} %param.6, f32[2048,2560]{0,1:T(8,128)} %fusion.44), kind=kOutput, calls=%fused_computation.53 | convolution fusion | flops 9428992000 | bytes 50200576 | tf_op jit(solution)/shard_map/dot_general | solution.py:444
  228.1 31.3 %fusion.5 = (bf16[2048,2560]{0,1:T(8,128)(2,1)}, bf16[2048,2560]{0,1:T(8,128)(2,1)}) fusion(f32[2048,2560]{0,1:T(8,128)} %fusion.44, f32[2048,2560]{0,1:T(8,128)} %fusion.46, bf16[2560,896]{1,0:T(8,128)(2,1)} %bitcast.142, bf16[1,2048,896]{2,1,0:T(8,128)(2,1)} %param.6), kind=kOutput, calls=%fused_computation.9 | convolution fusion | flops 9473884160 | bytes 71172096 | tf_op jit(solution)/shard_map/dot_general | solution.py:444
  259.4 15.3 %fusion.52 = bf16[2048,896]{0,1:T(8,128)(2,1)} fusion(bf16[896,2560]{1,0:T(8,128)(2,1)} %bitcast.140, bf16[2048,2560]{0,1:T(8,128)(2,1)} %get-tuple-element.42), kind=kOutput, calls=%fused_computation.92 | convolution fusion | flops 9395240960 | bytes 18743296 | tf_op jit(solution)/shard_map/dot_general | solution.py:444
  274.7 14.1 %convolution_convert_fusion.4 = bf16[896,2560]{1,0:T(8,128)(2,1)} fusion(bf16[2048,2560]{0,1:T(8,128)(2,1)} %get-tuple-element.42, bf16[2048,896]{0,1:T(8,128)(2,1)S(1)} %copy-done.6, f32[2048]{0:T(1024)S(1)} %get-tuple-element.54), kind=kOutput, calls=%fused_computation.55 | convolution fusion | flops 9403039744 | bytes 18751488 | tf_op jit(solution)/shard_map/dot_general | solution.py:444
  288.7 13.9 %convolution_convert_fusion.3 = bf16[896,2560]{1,0:T(8,128)(2,1)} fusion(bf16[2048,2560]{0,1:T(8,128)(2,1)} %get-tuple-element.41, bf16[2048,896]{0,1:T(8,128)(2,1)S(1)} %copy-done.6, f32[2048]{0:T(1024)S(1)} %get-tuple-element.54), kind=kOutput, calls=%fused_computation.54 | convolution fusion | flops 9403039744 | bytes 18751488 | tf_op jit(solution)/shard_map/dot_general | solution.py:444
  302.6 14.1 %fusion.29 = (f32[2048]{0:T(1024)S(1)}, bf16[2048,896]{0,1:T(8,128)(2,1)S(1)}) fusion(bf16[2048,896]{0,1:T(8,128)(2,1)S(1)} %copy-done.6, bf16[896,2560]{1,0:T(8,128)(2,1)S(1)} %bitcast.139, bf16[2048,2560]{0,1:T(8,128)(2,1)} %get-tuple-element.41, bf16[2048,896]{0,1:T(8,128)(2,1)} %fusion.52), kind=kOutput, calls=%fused_computation.47 | convolution fusion | flops 9411753984 | bytes 26091520 | tf_op jit(solution)/shard_map/dot_general | solution.py:444
  319.9 16.6 %convolution_convert_fusion.2 = bf16[2560,896]{1,0:T(8,128)(2,1)} fusion(bf16[2048,2560]{0,1:T(8,128)(2,1)} %get-tuple-element.55, bf16[2048,896]{0,1:T(8,128)(2,1)S(1)} %add_convert_fusion.2), kind=kOutput, calls=%fused_computation.52 | convolution fusion | flops 9397534720 | bytes 18743296 | tf_op jit(solution)/shard_map/dot_general | solution.py:444
  336.6 31.8 %fusion.2 = (bf16[2048,2560]{0,1:T(8,128)(2,1)}, bf16[2048,2560]{0,1:T(8,128)(2,1)}) fusion(f32[2048,2560]{0,1:T(8,128)} %fusion.38, f32[2048,2560]{0,1:T(8,128)} %get-tuple-element.56, bf16[2560,896]{1,0:T(8,128)(2,1)} %bitcast.135, bf16[2048,896]{0,1:T(8,128)(2,1)} %copy-done.3), kind=kOutput, calls=%fused_computation.4 | convolution fusion | flops 9473884160 | bytes 71172096 | tf_op jit(solution)/shard_map/dot_general | solution.py:444
  368.4 15.1 %convolution_convert_fusion.6 = bf16[896,2560]{1,0:T(8,128)(2,1)} fusion(bf16[2048,2560]{0,1:T(8,128)(2,1)} %get-tuple-element.40, bf16[1,2048,896]{1,2,0:T(8,128)(2,1)} %copy.33, f32[2048]{0:T(1024)S(1)} %copy-done.12), kind=kOutput, calls=%fused_computation.57 | convolution fusion | flops 9403039744 | bytes 18751488 | tf_op jit(solution)/shard_map/dot_general | solution.py:444
  383.5 15.1 %fusion.53 = bf16[2048,896]{0,1:T(8,128)(2,1)} fusion(bf16[896,2560]{1,0:T(8,128)(2,1)} %bitcast.133, bf16[2048,2560]{0,1:T(8,128)(2,1)} %get-tuple-element.40), kind=kOutput, calls=%fused_computation.93 | convolution fusion | flops 9395240960 | bytes 18743296 | tf_op jit(solution)/shard_map/dot_general | solution.py:444
  398.7 11.6 %convolution_convert_fusion.5 = bf16[896,2560]{1,0:T(8,128)(2,1)} fusion(bf16[2048,2560]{0,1:T(8,128)(2,1)S(1)} %bitcast.144, bf16[1,2048,896]{1,2,0:T(8,128)(2,1)S(1)} %copy-done.1, f32[2048]{0:T(1024)S(1)} %copy-done.12), kind=kOutput, calls=%fused_computation.56 | convolution fusion | flops 9403039744 | bytes 18751488 | tf_op jit(solution)/shard_map/dot_general | solution.py:444
  410.3 57.8 %scatter.2 = (bf16[56,1280]{1,0:T(8,128)(2,1)}, bf16[56,1280]{1,0:T(8,128)(2,1)}, bf16[80,896]{1,0:T(8,128)(2,1)}) custom-call(bf16[16,56,2560]{2,1,0:T(8,128)(2,1)} %bitcast.122, bf16[16,56,2560]{2,1,0:T(8,128)(2,1)} %bitcast.123, bf16[16,160,896]{2,1,0:T(8,128)(2,1)} %bitcast.121), custom_call_target="tpu_custom_call" | custom-call | tf_op jit(solution)/shard_map/scatter/pallas_call | solution.py:429
  469.1 60.1 %scatter.3 = (bf16[56,1280]{1,0:T(8,128)(2,1)}, bf16[56,1280]{1,0:T(8,128)(2,1)}, bf16[80,896]{1,0:T(8,128)(2,1)}) custom-call(bf16[16,56,2560]{2,1,0:T(8,128)(2,1)} %bitcast.119, bf16[16,56,2560]{2,1,0:T(8,128)(2,1)} %bitcast.120, bf16[16,160,896]{2,1,0:T(8,128)(2,1)} %bitcast.118), custom_call_target="tpu_custom_call" | custom-call | tf_op jit(solution)/shard_map/scatter/pallas_call | solution.py:429
  532.9 14.8 %fusion.22 = (f32[2048]{0:T(1024)S(1)}, bf16[2048,896]{0,1:T(8,128)(2,1)S(1)}) fusion(bf16[1,2048,896]{1,2,0:T(8,128)(2,1)S(1)} %copy-done.1, bf16[896,2560]{1,0:T(8,128)(2,1)} %bitcast.131, bf16[2048,2560]{0,1:T(8,128)(2,1)} %get-tuple-element.39, bf16[2048,896]{0,1:T(8,128)(2,1)} %fusion.53), kind=kOutput, calls=%fused_computation.40 | convolution fusion | flops 9411753984 | bytes 26091520 | tf_op jit(solution)/shard_map/dot_general | solution.py:444
  551.9 6.1 %copy.45 = bf16[1,2048,896]{2,1,0:T(8,128)(2,1)} copy(bf16[1,2048,896]{1,2,0:T(8,128)(2,1)} %fusion.31) | data formatting | bytes 7340032
  (67 shorter events, 25.5 us)
Async XLA Ops:
  2.4 18.8 %collective-permute-start = (bf16[2,2,28,2560]{3,1,2,0:T(2,128)(2,1)S(1)}, bf16[2,2,28,2560]{3,1,2,0:T(2,128)(2,1)S(1)}, u32[]{:S(2)}, u32[]{:S(2)}) collective-permute-start(bf16[2,2,28,2560]{3,1,2,0:T(2,128)(2,1)S(1)} %copy.30), channel_id=1, source_target_pairs={{0,1},{1,0},{2,3},{3,2},{4,5},{5,4},{6,7},{7,6},{8,9},{9,8},{10,11... | collective-permute-start | bytes 1720328 | tf_op jit(solution)/shard_map/ppermute | solution.py:473
  10.6 9.1 %copy-start.7 = (bf16[2,80,896]{2,1,0:T(8,128)(2,1)S(1)}, bf16[2,80,896]{2,1,0:T(8,128)(2,1)}, u32[]{:S(2)}) copy-start(bf16[2,80,896]{2,1,0:T(8,128)(2,1)} %param.9) | copy-start | bytes 860164
  20.4 67.5 %copy-start.11 = (f32[2048]{0:T(1024)}, f32[2048]{0:T(1024)S(1)}, u32[]{:S(2)}) copy-start(f32[2048]{0:T(1024)S(1)} %get-tuple-element.52) | copy-start | bytes 24580
  69.8 18.1 %copy-start = (bf16[1,2048,896]{1,2,0:T(8,128)(2,1)S(1)}, bf16[1,2048,896]{1,2,0:T(8,128)(2,1)}, u32[]{:S(2)}) copy-start(bf16[1,2048,896]{1,2,0:T(8,128)(2,1)} %copy.33) | copy-start | bytes 11010052
  173.1 19.0 %copy-start.5 = (bf16[2048,896]{0,1:T(8,128)(2,1)S(1)}, bf16[2048,896]{0,1:T(8,128)(2,1)}, u32[]{:S(2)}) copy-start(bf16[2048,896]{0,1:T(8,128)(2,1)} %get-tuple-element.58) | copy-start | bytes 11010052
  173.1 19.0 %copy-start.14 = (bf16[16,56,2560]{2,1,0:T(8,128)(2,1)S(1)}, bf16[16,56,2560]{2,1,0:T(8,128)(2,1)}, u32[]{:S(2)}) copy-start(bf16[16,56,2560]{2,1,0:T(8,128)(2,1)} %get-tuple-element.21) | copy-start | bytes 13762564
  259.4 15.3 %copy-start.6 = (bf16[2048,896]{0,1:T(8,128)(2,1)S(1)}, bf16[2048,896]{0,1:T(8,128)(2,1)}, u32[]{:S(2)}) copy-start(bf16[2048,896]{0,1:T(8,128)(2,1)} %get-tuple-element.58) | copy-start | bytes 11010052
  274.7 27.9 %slice-start = ((s8[4587520]{0:T(1024)(128)(4,1)}), s8[4194304]{0:T(1024)(128)(4,1)S(1)}, s32[]{:S(2)}) async-start(s8[4587520]{0:T(1024)(128)(4,1)} %bitcast.137), calls=%async_computation | async-start | bytes 8388608
  288.7 13.9 %slice-start.1 = ((s8[4587520]{0:T(1024)(128)(4,1)}), s8[393216]{0:T(1024)(128)(4,1)S(1)}, s32[]{:S(2)}) async-start(s8[4587520]{0:T(1024)(128)(4,1)} %bitcast.137), calls=%async_computation.1 | async-start | bytes 786432
  302.6 14.1 %copy-start.2 = (bf16[1,2048,896]{1,2,0:T(8,128)(2,1)S(1)}, bf16[1,2048,896]{1,2,0:T(8,128)(2,1)}, u32[]{:S(2)}) copy-start(bf16[1,2048,896]{1,2,0:T(8,128)(2,1)} %copy.27) | copy-start | bytes 11010052
  302.6 14.1 %copy-start.13 = (f32[2048]{0:T(1024)S(1)}, f32[2048]{0:T(1024)}, u32[]{:S(2)}) copy-start(f32[2048]{0:T(1024)} %get-tuple-element.53) | copy-start | bytes 24580
  319.9 16.6 %copy-start.3 = (bf16[2048,896]{0,1:T(8,128)(2,1)}, bf16[2048,896]{0,1:T(8,128)(2,1)S(1)}, u32[]{:S(2)}) copy-start(bf16[2048,896]{0,1:T(8,128)(2,1)S(1)} %add_convert_fusion.2) | copy-start | bytes 11010052
  336.6 31.8 %copy-start.12 = (f32[2048]{0:T(1024)S(1)}, f32[2048]{0:T(1024)}, u32[]{:S(2)}) copy-start(f32[2048]{0:T(1024)} %copy-done.11) | copy-start | bytes 24580
  368.4 30.2 %slice-start.2 = ((s8[10485760]{0:T(1024)(128)(4,1)}), s8[4194304]{0:T(1024)(128)(4,1)S(1)}, s32[]{:S(2)}) async-start(s8[10485760]{0:T(1024)(128)(4,1)} %bitcast.143), calls=%async_computation.2 | async-start | bytes 8388608
  368.4 30.2 %slice-start.3 = ((s8[10485760]{0:T(1024)(128)(4,1)}), s8[4194304]{0:T(1024)(128)(4,1)S(1)}, s32[]{:S(2)}) async-start(s8[10485760]{0:T(1024)(128)(4,1)} %bitcast.143), calls=%async_computation.3 | async-start | bytes 8388608
  383.5 15.1 %copy-start.1 = (bf16[1,2048,896]{1,2,0:T(8,128)(2,1)S(1)}, bf16[1,2048,896]{1,2,0:T(8,128)(2,1)}, u32[]{:S(2)}) copy-start(bf16[1,2048,896]{1,2,0:T(8,128)(2,1)} %copy.33) | copy-start | bytes 11010052
  383.5 15.1 %slice-start.4 = ((s8[10485760]{0:T(1024)(128)(4,1)}), s8[2097152]{0:T(1024)(128)(4,1)S(1)}, s32[]{:S(2)}) async-start(s8[10485760]{0:T(1024)(128)(4,1)} %bitcast.143), calls=%async_computation.4 | async-start | bytes 4194304
  530.4 17.3 %copy-start.4 = (bf16[2048,896]{0,1:T(8,128)(2,1)S(1)}, bf16[2048,896]{0,1:T(8,128)(2,1)}, u32[]{:S(2)}) copy-start(bf16[2048,896]{0,1:T(8,128)(2,1)} %copy-done.3) | copy-start | bytes 11010052
  530.4 17.3 %copy-start.10 = (f32[2048]{0:T(1024)S(1)}, f32[2048]{0:T(1024)}, u32[]{:S(2)}) copy-start(f32[2048]{0:T(1024)} %get-tuple-element.51) | copy-start | bytes 24580
  530.4 28.3 %collective-permute-start.1 = (bf16[2,2,28,1280]{3,2,0,1:T(8,128)(2,1)S(1)}, bf16[2,2,28,1280]{3,2,0,1:T(8,128)(2,1)S(1)}, u32[]{:S(2)}, u32[]{:S(2)}) collective-permute-start(bf16[2,2,28,1280]{3,2,0,1:T(8,128)(2,1)S(1)} %get-tuple-element.36), channel_id=1, source_target_pairs={{0,1},{1,0},{2,3},{3,2},{4,5},{5,4},{6,7},{7,6},{8,9},{9,8},{10,11... | collective-permute-start | bytes 860168 | tf_op jit(solution)/shard_map/ppermute | solution.py:513
  551.8 6.1 %copy-start.8 = (bf16[80,896]{1,0:T(8,128)(2,1)S(1)}, bf16[80,896]{1,0:T(8,128)(2,1)}, u32[]{:S(2)}) copy-start(bf16[80,896]{1,0:T(8,128)(2,1)} %get-tuple-element.26) | copy-start | bytes 430084
  551.9 6.1 %copy-start.9 = (bf16[80,896]{1,0:T(8,128)(2,1)S(1)}, bf16[80,896]{1,0:T(8,128)(2,1)}, u32[]{:S(2)}) copy-start(bf16[80,896]{1,0:T(8,128)(2,1)} %get-tuple-element.27) | copy-start | bytes 430084

commit v2 on v1

--- a/solution.py
+++ b/solution.py
@@ -177,32 +177,42 @@
         block = part(p, self.split, self.full, 0, p.core)
         half = [part(p, self.split, self.full, 0, p.core, h) for h in (0, 1)]
         theirs = part(p, self.split, self.full, 0, 1 - p.core)
-        for base in (0, 4, 8, 12, 16):
+        def ring(i, _):
+            base = 4 * i
             wait_send(base, block)
             wait_send(base + 1, block)
             wait_send(base + 2, half[0])
             wait_send(base + 3, half[1])
-        for slot in range(20, 36):
+            return 0
+
+        def across(slot, _):
             wait_send(slot, block)
             remote(theirs, theirs, self.send.at[slot], self.recv.at[slot], p.partner()).wait_recv()
-
-    def steps(self):
-        return (
-            [self.first, self.second, self.third]
-            + [functools.partial(self.relay, k) for k in range(4)]
-            + [functools.partial(self.last, k) for k in range(4)]
-            + [self.finish]
-        )
-
-
-def woven(lists, lag):
-    out = []
-    longest = max(len(l) for l in lists)
-    for t in range(longest + lag * (len(lists) - 1)):
-        for i, l in enumerate(lists):
-            if 0 <= t - lag * i < len(l):
-                out.append(l[t - lag * i])
-    return out
+            return 0
+
+        lax.fori_loop(0, 5, ring, 0)
+        lax.fori_loop(20, 36, across, 0)
+
+    def timed(self, i, stage, sem):
+        relay = [functools.partial(self.relay, k) for k in range(4)]
+        last = [functools.partial(self.last, k) for k in range(4)]
+        return [
+            (0, functools.partial(self.keep_in, stage, sem)),
+            (0, self.first),
+            (1, functools.partial(self.keep_out, stage, sem)),
+            (3 + i, self.second),
+            (6 + i, relay[0]),
+            (7 + i, self.third),
+            (9 + i, relay[1]),
+            (11 + i, relay[2]),
+            (13 + i, last[0]),
+            (14 + i, relay[3]),
+            (16 + i, last[1]),
+            (18 + i, last[2]),
+            (20 + i, last[3]),
+            (23, self.finish),
+            (23, functools.partial(self.kept, stage, sem)),
+        ]
 
 
 def gather_kernel(side, splits, *refs):
@@ -210,15 +220,8 @@
     own, full, (stage, send, recv, local) = refs[:n], refs[n : 2 * n], (refs[2 * n : 3 * n], *refs[3 * n :])
     place = Place(side)
     greet(place)
-    gathers = [Gather(place, s, o, f, send.at[i], recv.at[i]) for i, (s, o, f) in enumerate(zip(splits, own, full))]
-    steps = [functools.partial(g.keep_in, stage[i], local.at[i]) for i, g in enumerate(gathers)]
-    woven_steps = woven([g.steps() for g in gathers], 1)
-    steps += woven_steps[: 2 * n]
-    steps += [functools.partial(g.keep_out, stage[i], local.at[i]) for i, g in enumerate(gathers)]
-    steps += woven_steps[2 * n :]
-    steps += [functools.partial(g.kept, stage[i], local.at[i]) for i, g in enumerate(gathers)]
-    for step in steps:
-        step()
+    for _, event in sorted(gather_events(place, splits, own, full, stage, send, recv, local), key=lambda e: e[0]):
+        event()
 
 
 def gather(side, chips, splits, blocks, collective_id):
@@ -258,47 +261,57 @@
             pltpu.VMEM((2, h, w), BF16),
         ]
 
-    def __init__(self, place, split, terms, out, bufs, send, recv):
+    def __init__(self, place, split, terms, out, bufs, send, recv, near=False):
+        self.near = near
         self.place, self.split, self.terms, self.out, self.send, self.recv = place, split, terms, out, send, recv
         self.sums, self.theirs, self.h0, self.h1, self.full, self.g0, self.g1, self.last_in = bufs
         self.w = self.sums.shape[-1]
         (_, self.w0), (_, self.w1) = halves(self.w)
 
-    def copies(self):
+    def start(self):
         p, n = self.place, self.place.side
         other = 1 - p.core
-        for b in range(n):
-            for a in range(n):
+        for k in (2, 1, -1, 0):
+
+            def send(a, _, k=k):
+                b = p.step(p.a, k)
                 slot = b * n + a
-                mine = pltpu.make_async_copy(
-                    part(p, self.split, self.terms, p.chip(a, b), p.core), self.sums.at[b, a], self.send.at[16 + slot]
-                )
-                sent = remote(
+                remote(
                     part(p, self.split, self.terms, p.chip(a, b, other), other),
                     self.theirs.at[b, a],
                     self.send.at[slot],
                     self.recv.at[slot],
                     p.partner(),
-                )
-                yield b, a, mine, sent
-
-    def start(self):
-        for _, _, mine, sent in self.copies():
-            sent.start()
-            mine.start()
+                ).start()
+                if not self.near:
+                    b = p.step(p.b, k)
+                    pltpu.make_async_copy(
+                        part(p, self.split, self.terms, p.chip(a, b), p.core),
+                        self.sums.at[b, a],
+                        self.send.at[16 + b * n + a],
+                    ).start()
+                return 0
+
+            lax.fori_loop(0, n, send, 0)
 
     def pair(self, k):
         p = self.place
         b = p.step(p.b, k)
-        for a in range(p.side):
+
+        def add(a, _):
             slot = b * p.side + a
-            pltpu.make_async_copy(
-                self.sums.at[b, a], self.sums.at[b, a], self.send.at[16 + slot]
-            ).wait()
+            mine = self.sums.at[b, a]
+            if self.near:
+                mine = part(p, self.split, self.terms, p.chip(a, b), p.core)
+            else:
+                pltpu.make_async_copy(mine, mine, self.send.at[16 + slot]).wait()
             remote(
                 self.sums.at[b, a], self.theirs.at[b, a], self.send.at[slot], self.recv.at[slot], p.partner()
-            ).wait()
-            self.sums[b, a] = (self.sums[b, a].astype(F32) + self.theirs[b, a].astype(F32)).astype(BF16)
+            ).wait_recv()
+            self.sums[b, a] = (mine[...].astype(F32) + self.theirs[b, a].astype(F32)).astype(BF16)
+            return 0
+
+        lax.fori_loop(0, p.side, add, 0)
 
     def ring_b(self, slot, b, src, dst, by):
         return remote(src, dst, self.send.at[32 + slot], self.recv.at[32 + slot], self.place.b_next(by))
@@ -329,16 +342,23 @@
         c = self.b_copies()
         c[0].wait_recv()
         right, left = p.step(p.b, 1), p.step(p.b, -1)
-        for a in range(n):
+
+        def add_low(a, _):
             self.sums[right, a, :, : self.w0] = (
                 self.sums[right, a, :, : self.w0].astype(F32) + self.h0[a].astype(F32)
             ).astype(BF16)
-        c[2].start()
-        c[1].wait_recv()
-        for a in range(n):
+            return 0
+
+        def add_high(a, _):
             self.sums[left, a, :, self.w0 :] = (
                 self.sums[left, a, :, self.w0 :].astype(F32) + self.h1[a].astype(F32)
             ).astype(BF16)
+            return 0
+
+        lax.fori_loop(0, n, add_low, 0)
+        c[2].start()
+        c[1].wait_recv()
+        lax.fori_loop(0, n, add_high, 0)
         c[3].start()
 
     def a_copies(self):
@@ -359,10 +379,14 @@
         c = self.b_copies()
         c[2].wait_recv()
         c[3].wait_recv()
-        for a in range(n):
+
+        def add(a, _):
             self.theirs[0, a] = (
                 self.sums[p.b, a].astype(F32) + self.full[0, a].astype(F32) + self.full[1, a].astype(F32)
             ).astype(BF16)
+            return 0
+
+        lax.fori_loop(0, n, add, 0)
         c = self.a_copies()
         c[0].start()
         c[1].start()
@@ -393,8 +417,15 @@
         for copy in (*self.b_copies(), *c):
             copy.wait_send()
 
-    def steps(self):
-        return [
+        def sent(slot, _):
+            first = self.theirs.at[0, 0]
+            remote(self.sums.at[0, 0], first, self.send.at[slot], self.recv.at[slot], p.partner()).wait_send()
+            return 0
+
+        lax.fori_loop(0, p.side * p.side, sent, 0)
+
+    def timed(self, base, times):
+        steps = (
             self.start,
             functools.partial(self.pair, 2),
             self.b_out,
@@ -405,55 +436,361 @@
             self.b_in,
             self.a_relay,
             self.finish,
+        )
+        return [(base + t, s) for t, s in zip(times, steps)]
+
+
+TILE, CHUNK, SUB = 512, 512, 256
+BIG, PART = 1024, 512
+
+
+def scaled(h):
+    wide = h.astype(F32)
+    return wide, lax.rsqrt(jnp.mean(wide**2, -1, keepdims=True) + 1e-6)
+
+
+def normed(h):
+    wide, scale = scaled(h)
+    return (wide * scale).astype(BF16)
+
+
+def state_back(h, g, da):
+    wide, scale = scaled(h)
+    ct = da.astype(F32)
+    inner = jnp.sum(ct * wide, -1, keepdims=True)
+    by_h = (ct * scale - wide * (scale**3) * inner / h.shape[-1]).astype(BF16)
+    return (g.astype(F32) + by_h.astype(F32)).astype(BF16)
+
+
+def parts_of(t, tile, sub):
+    return [pl.ds(pl.multiple_of(t * tile + i * sub, sub), sub) for i in range(tile // sub)]
+
+
+ANY = pl.BlockSpec(memory_space=pl.ANY)
+
+
+def dot(a, w, dims=((1,), (0,))):
+    return lax.dot_general(a, w, (dims, ((), ())), preferred_element_type=F32)
+
+
+def run_at(slot, slots, events, span=None):
+    span = span or slots
+    events = [(min(t * slots // span, slots - 1), e) for t, e in sorted(events, key=lambda e: e[0])]
+    for s in sorted({t for t, _ in events}):
+
+        @pl.when(slot == s)
+        def _(s=s):
+            for t, event in events:
+                if t == s:
+                    event()
+
+
+def gather_events(place, splits, own, full, stage, send, recv, local):
+    events = []
+    for i, (split, o, f) in enumerate(zip(splits, own, full)):
+        events += Gather(place, split, o, f, send.at[i], recv.at[i]).timed(i, stage[i], local.at[i])
+    return events
+
+
+def gather_scratch(splits, blocks):
+    n = len(splits)
+    return [pltpu.VMEM(block_shape(s, *b.shape[1:]), b.dtype) for s, b in zip(splits, blocks)] + [
+        pltpu.SemaphoreType.DMA((n, Gather.COPIES)),
+        pltpu.SemaphoreType.DMA((n, Gather.COPIES)),
+        pltpu.SemaphoreType.DMA((n,)),
+    ]
+
+
+def forward_kernel(side, splits, chunks, tiles, x_ref, wg_ref, wu_ref, wd_ref, *refs):
+    n = len(splits)
+    own, (h_ref, gate_ref, up_ref, at_ref), refs = refs[:n], refs[n : n + 4], refs[n + 4 :]
+    full, (p_ref, a_ref), stage, (send, recv, local) = refs[:n], refs[n : n + 2], refs[n + 2 : 2 * n + 2], refs[2 * n + 2 :]
+    place = Place(side)
+    c, t = pl.program_id(0), pl.program_id(1)
+    events = [(0, functools.partial(greet, place))] + gather_events(place, splits, own, full, stage, send, recv, local)
+    run_at(c * tiles + t, (chunks + 1) * tiles, events, 24)
+    rows = pl.ds(pl.multiple_of(t * TILE, TILE), TILE)
+
+    @pl.when(c == 0)
+    def _():
+        a = normed(x_ref[rows, :])
+        a_ref[rows, :] = a
+        at_ref[...] = a.T
+
+    @pl.when(c < chunks)
+    def _():
+        columns = pl.ds(pl.multiple_of(c * CHUNK, CHUNK), CHUNK)
+        for i, part_rows in enumerate(parts_of(t, TILE, SUB)):
+            a = a_ref[part_rows, :]
+            gate = dot(a, wg_ref[...])
+            up = dot(a, wu_ref[...])
+            gate_ref[i * SUB : (i + 1) * SUB, :] = gate
+            up_ref[i * SUB : (i + 1) * SUB, :] = up
+            p_ref[part_rows, columns] = (gate * jax.nn.sigmoid(gate) * up).astype(BF16)
+
+    @pl.when(c == chunks)
+    def _():
+        down = dot(p_ref[rows, :], wd_ref[...]).astype(BF16)
+        h_ref[...] = (x_ref[rows, :].astype(F32) + down.astype(F32)).astype(BF16)
+
+
+def forward(side, chips, splits, x, weights, blocks, collective_id):
+    tokens, d = x.shape
+    ff = weights[0].shape[1]
+    n, chunks, tiles = len(splits), ff // CHUNK, tokens // TILE
+    last = chunks - 1
+    wide = pl.BlockSpec((d, CHUNK), lambda c, t: (0, jnp.minimum(c, last)))
+    tile = pl.BlockSpec((TILE, d), lambda c, t: (jnp.where(c == chunks, t, 0), 0))
+    kept = pl.BlockSpec((TILE, CHUNK), lambda c, t: (jnp.where(c == chunks, tiles - 1, t), jnp.minimum(c, last)))
+    turned = pl.BlockSpec((d, TILE), lambda c, t: (0, jnp.where(c == 0, t, tiles - 1)))
+    out = pl.pallas_call(
+        functools.partial(forward_kernel, side, splits, chunks, tiles),
+        grid=(chunks + 1, tiles),
+        out_shape=[
+            jax.ShapeDtypeStruct(x.shape, BF16),
+            jax.ShapeDtypeStruct((tokens, ff), F32),
+            jax.ShapeDtypeStruct((tokens, ff), F32),
+            jax.ShapeDtypeStruct((d, tokens), BF16),
         ]
-
-
-def scatter_kernel(side, splits, *refs):
+        + [jax.ShapeDtypeStruct((chips, *b.shape[1:]), b.dtype) for b in blocks],
+        in_specs=[
+            pl.BlockSpec((tokens, d), lambda c, t: (0, 0), pipeline_mode=pl.Buffered(1)),
+            wide,
+            wide,
+            pl.BlockSpec((ff, d), lambda c, t: (0, 0), pipeline_mode=pl.Buffered(1)),
+        ]
+        + [ANY] * n,
+        out_specs=[tile, kept, kept, turned] + [ANY] * n,
+        scratch_shapes=[pltpu.VMEM((tokens, ff), BF16), pltpu.VMEM((tokens, d), BF16)] + gather_scratch(splits, blocks),
+        compiler_params=pltpu.CompilerParams(
+            collective_id=collective_id, has_side_effects=True, vmem_limit_bytes=60 * 2**20,
+            dimension_semantics=("arbitrary", "arbitrary"),
+        ),
+        name="forward",
+    )(x, *weights, *blocks)
+    return out[0], out[1:4], out[4:]
+
+
+def top_kernel(chunks, tiles, h_ref, g_ref, wg_ref, wu_ref, wd_ref, *refs):
+    by_gate, by_up, by_down, da_ref, acc, p_ref, dg_ref, du_ref, da_stage, at_ref, a_ref, da_sem = refs
+    c, t = pl.program_id(0), pl.program_id(1)
+
+    rows = pl.ds(pl.multiple_of(t * BIG, BIG), BIG)
+
+    @pl.when((t < tiles) & (c == 0))
+    def _():
+        a = normed(h_ref[rows, :])
+        a_ref[rows, :] = a
+        at_ref[:, rows] = a.T
+
+    @pl.when(t < tiles)
+    def _():
+        def some(i, _):
+            r = pl.ds(pl.multiple_of(t * BIG + i * PART, PART), PART)
+            a, g = a_ref[r, :], g_ref[r, :]
+            gate, up, dp = dot(a, wg_ref[...]), dot(a, wu_ref[...]), d_hidden(g, wd_ref)
+            p_ref[r, :], dg_ref[r, :], du_ref[r, :] = add_da(c, r, gate, up, dp, wg_ref, wu_ref, acc)
+            return 0
+
+        lax.fori_loop(0, BIG // PART, some, 0)
+
+    @pl.when((t < tiles) & (c == chunks - 1))
+    def _():
+        da_stage[rows, :] = state_back(h_ref[rows, :], g_ref[rows, :], acc[rows, :].astype(BF16))
+
+    @pl.when(t == tiles)
+    def _():
+        by_down[...] = dot(p_ref[...], g_ref[...], ((0,), (0,))).astype(BF16)
+
+    @pl.when(t == tiles + 1)
+    def _():
+        by_gate[...] = dot(at_ref[...], dg_ref[...]).astype(BF16)
+
+    @pl.when(t == tiles + 2)
+    def _():
+        by_up[...] = dot(at_ref[...], du_ref[...]).astype(BF16)
+
+        @pl.when(c == chunks - 1)
+        def _():
+            copy = pltpu.make_async_copy(da_stage, da_ref, da_sem)
+            copy.start()
+            copy.wait()
+
+
+def d_hidden(g, wd_ref):
+    return dot(g, wd_ref[...], ((1,), (1,))).astype(BF16).astype(F32)
+
+
+def add_da(c, rows, gate, up, dp, wg_ref, wu_ref, acc):
+    sig = jax.nn.sigmoid(gate)
+    act = gate * sig
+    d_gate = (dp * up * (sig * (1 + gate * (1 - sig)))).astype(BF16)
+    d_up = (dp * act).astype(BF16)
+    da = dot(d_gate, wg_ref[...], ((1,), (1,))) + dot(d_up, wu_ref[...], ((1,), (1,)))
+    acc[rows, :] = jnp.where(c == 0, 0.0, acc[rows, :]) + da
+    return (act * up).astype(BF16), d_gate, d_up
+
+
+def top(h, g, weights):
+    tokens, d = h.shape
+    ff = weights[0].shape[1]
+    chunks, tiles = ff // CHUNK, tokens // BIG
+    whole = pl.BlockSpec((tokens, d), lambda c, t: (0, 0), pipeline_mode=pl.Buffered(1))
+    wide = pl.BlockSpec((d, CHUNK), lambda c, t: (0, c))
+    tall = pl.BlockSpec((CHUNK, d), lambda c, t: (c, 0))
+    shape = jax.ShapeDtypeStruct
+    out = pl.pallas_call(
+        functools.partial(top_kernel, chunks, tiles),
+        grid=(chunks, tiles + 3),
+        out_shape=[shape((d, ff), BF16), shape((d, ff), BF16), shape((ff, d), BF16), shape((tokens, d), BF16)],
+        in_specs=[whole, whole, wide, wide, tall],
+        out_specs=[wide, wide, tall, ANY],
+        scratch_shapes=[pltpu.VMEM((tokens, d), F32)]
+        + [pltpu.VMEM((tokens, CHUNK), BF16)] * 3
+        + [pltpu.VMEM((tokens, d), BF16), pltpu.VMEM((d, tokens), BF16)]
+        + [pltpu.VMEM((tokens, d), BF16), pltpu.SemaphoreType.DMA(())],
+        compiler_params=pltpu.CompilerParams(
+            vmem_limit_bytes=60 * 2**20, dimension_semantics=("arbitrary", "arbitrary")
+        ),
+        name="top",
+    )(h, g, *weights)
+    return out[:3], out[3]
+
+
+def lower_kernel(side, splits, chunks, tiles, h_ref, g_ref, gate_ref, up_ref, wg_ref, wu_ref, wd_ref, *refs):
     n = len(splits)
-    terms, outs, bufs, (send, recv) = refs[:n], refs[n : 2 * n], refs[2 * n : 10 * n], refs[10 * n :]
+    terms, (by_down, da_ref, dg_ref, du_ref), refs = refs[:n], refs[n : n + 4], refs[n + 4 :]
+    outs, (acc, p_ref, da_stage, da_sem), refs = refs[:n], refs[n : n + 4], refs[n + 4 :]
+    bufs, (send, recv) = refs[: 8 * n], refs[8 * n :]
+    c, t = pl.program_id(0), pl.program_id(1)
     place = Place(side)
-    greet(place)
-    scatters = [
-        Scatter(place, splits[i], terms[i], outs[i], bufs[8 * i : 8 * i + 8], send.at[i], recv.at[i]) for i in range(n)
-    ]
-    lists = [s.steps() for s in scatters]
-    for l in lists:
-        l.pop(0)()
-    for step in woven(lists, 2):
-        step()
-
-
-def scatter(side, splits, terms, collective_id):
-    n = len(splits)
-    shapes = [block_shape(s, *t.shape[1:]) for s, t in zip(splits, terms)]
-    return pl.pallas_call(
-        functools.partial(scatter_kernel, side, splits),
-        out_shape=[jax.ShapeDtypeStruct(s, BF16) for s in shapes],
-        in_specs=[pl.BlockSpec(memory_space=pl.ANY)] * n,
-        out_specs=[pl.BlockSpec(memory_space=pltpu.VMEM)] * n,
-        scratch_shapes=[b for s, t in zip(splits, terms) for b in Scatter.scratch(side, s, *t.shape[1:])]
+    events = [(0, functools.partial(greet, place))]
+    for i in range(n):
+        s = Scatter(place, splits[i], terms[i], outs[i], bufs[8 * i : 8 * i + 8], send.at[i], recv.at[i])
+        events += s.timed(0, [0] + [4 * i + k for k in (2, 2, 3, 3, 4, 6, 10, 12, 14)])
+    run_at(c * (tiles + 1) + t, chunks * (tiles + 1), events)
+
+    rows = pl.ds(pl.multiple_of(t * TILE, TILE), TILE)
+
+    @pl.when(t < tiles)
+    def _():
+        parts = parts_of(t, TILE, SUB)
+        dps = [d_hidden(g_ref[r, :], wd_ref) for r in parts]
+        for i, (r, dp) in enumerate(zip(parts, dps)):
+            here = slice(i * SUB, (i + 1) * SUB)
+            p_ref[r, :], dg_ref[here, :], du_ref[here, :] = add_da(
+                c, r, gate_ref[here, :], up_ref[here, :], dp, wg_ref, wu_ref, acc
+            )
+
+    @pl.when((t < tiles) & (c == chunks - 1))
+    def _():
+        da_stage[rows, :] = state_back(h_ref[rows, :], g_ref[rows, :], acc[rows, :].astype(BF16))
+
+    @pl.when(t == tiles)
+    def _():
+        by_down[...] = dot(p_ref[...], g_ref[...], ((0,), (0,))).astype(BF16)
+
+        @pl.when(c == chunks - 1)
+        def _():
+            copy = pltpu.make_async_copy(da_stage, da_ref, da_sem)
+            copy.start()
+            copy.wait()
+
+
+def lower(side, splits, kept, h, g, weights, terms, collective_id):
+    tokens, d = g.shape
+    ff = weights[0].shape[1]
+    n, chunks, tiles = len(terms), ff // CHUNK, tokens // TILE
+    whole = pl.BlockSpec((tokens, d), lambda c, t: (0, 0), pipeline_mode=pl.Buffered(1))
+    wide = pl.BlockSpec((d, CHUNK), lambda c, t: (0, c))
+    tall = pl.BlockSpec((CHUNK, d), lambda c, t: (c, 0))
+    tile = pl.BlockSpec((TILE, CHUNK), lambda c, t: (jnp.minimum(t, tiles - 1), c))
+    shape = jax.ShapeDtypeStruct
+    out = pl.pallas_call(
+        functools.partial(lower_kernel, side, splits, chunks, tiles),
+        grid=(chunks, tiles + 1),
+        out_shape=[shape((ff, d), BF16), shape((tokens, d), BF16), shape((tokens, ff), BF16), shape((tokens, ff), BF16)]
+        + [shape(block_shape(s, *t.shape[1:]), BF16) for s, t in zip(splits, terms)],
+        in_specs=[whole, whole, tile, tile, wide, wide, tall] + [ANY] * n,
+        out_specs=[tall, ANY, tile, tile]
+        + [pl.BlockSpec(block_shape(s, *t.shape[1:]), lambda c, t: (0, 0)) for s, t in zip(splits, terms)],
+        scratch_shapes=[
+            pltpu.VMEM((tokens, d), F32),
+            pltpu.VMEM((tokens, CHUNK), BF16),
+            pltpu.VMEM((tokens, d), BF16),
+            pltpu.SemaphoreType.DMA(()),
+        ]
+        + [b for s, t in zip(splits, terms) for b in Scatter.scratch(side, s, *t.shape[1:])]
         + [pltpu.SemaphoreType.DMA((n, Scatter.SEMS)), pltpu.SemaphoreType.DMA((n, Scatter.SEMS))],
         compiler_params=pltpu.CompilerParams(
-            collective_id=collective_id, has_side_effects=True, vmem_limit_bytes=56 * 2**20
+            collective_id=collective_id,
+            has_side_effects=True,
+            vmem_limit_bytes=67043328,
+            dimension_semantics=("arbitrary", "arbitrary"),
         ),
-        name="scatter",
-    )(*terms)
-
-
-def dot(a, w, dims=((1,), (0,))):
-    return lax.dot_general(a, w, (dims, ((), ())), preferred_element_type=F32)
-
-
-def normed(h):
-    wide = h.astype(F32)
-    scale = lax.rsqrt(jnp.mean(wide**2, -1, keepdims=True) + 1e-6)
-    return (wide * scale).astype(BF16), scale
-
-
-def norm_back(h, scale, da):
-    wide, ct = h.astype(F32), da.astype(F32)
-    inner = jnp.sum(ct * wide, -1, keepdims=True)
-    return (ct * scale - wide * (scale**3) * inner / h.shape[-1]).astype(BF16)
+        name="lower",
+    )(h, g, *kept, *weights, *terms)
+    return out[0], out[1], out[2:4], out[4:]
+
+
+PIECES = 4
+
+
+def wide_kernel(side, at_ref, dg_ref, du_ref, down_ref, *refs):
+    outs, terms, bufs, (send, recv) = refs[:5], refs[5:9], refs[9:49], refs[49:]
+    slot = pl.program_id(0)
+    place = Place(side)
+    sources, splits = (down_ref, *terms), ("rows",) + ("columns",) * 4
+    events = [(0, functools.partial(greet, place))]
+    for i in range(5):
+        s = Scatter(
+            place, splits[i], sources[i], outs[i], bufs[8 * i : 8 * i + 8], send.at[i], recv.at[i], near=i > 0
+        )
+        times = (0, 4, 5, 6, 7, 8, 11, 17, 22, 26) if i == 0 else (0, 2, 3, 4, 5, 6, 9, 14, 18, 22)
+        events += s.timed(2 * PIECES * i, times)
+    run_at(slot, 8 * PIECES + 1, events)
+    chips, height, _ = terms[0].shape
+    some = chips // PIECES
+    for i in range(4):
+
+        @pl.when(slot // (2 * PIECES) == i)
+        def _(i=i):
+            q = slot // 2 % PIECES
+            width = terms[i].shape[-1] // 2
+            columns = pl.ds(pl.multiple_of(slot % 2 * width, 128), width)
+            rows = pl.ds(pl.multiple_of(q * some * height, some * height), some * height)
+            got = dot(at_ref[rows, :], (dg_ref, du_ref)[i // 2][:, columns])
+            terms[i][pl.ds(q * some, some), :, columns] = got.reshape(some, height, got.shape[-1]).astype(BF16)
+
+
+def wide_grads(side, chips, at, hidden, down, collective_id):
+    d, tokens = at.shape
+    ff = hidden[0].shape[1]
+    half, height = ff // 2, d // chips
+    shapes = [block_shape("rows", *down.shape[1:])] + [block_shape("columns", height, half)] * 4
+    splits, sizes = ("rows",) + ("columns",) * 4, [down.shape[1:]] + [(height, half)] * 4
+    return pl.pallas_call(
+        functools.partial(wide_kernel, side),
+        grid=(8 * PIECES + 1,),
+        out_shape=[jax.ShapeDtypeStruct(s, BF16) for s in shapes],
+        in_specs=[
+            pl.BlockSpec((d, tokens), lambda s: (0, 0), pipeline_mode=pl.Buffered(1)),
+            pl.BlockSpec((tokens, half), lambda s: (0, jnp.minimum(s // (2 * PIECES), 1))),
+            pl.BlockSpec((tokens, half), lambda s: (0, jnp.clip(s // (2 * PIECES) - 2, 0, 1))),
+            ANY,
+        ],
+        out_specs=[pl.BlockSpec(s, lambda i: (0, 0)) for s in shapes],
+        scratch_shapes=[pltpu.VMEM((chips, height, half), BF16)] * 4
+        + [b for s, z in zip(splits, sizes) for b in Scatter.scratch(side, s, *z)]
+        + [pltpu.SemaphoreType.DMA((5, Scatter.SEMS)), pltpu.SemaphoreType.DMA((5, Scatter.SEMS))],
+        compiler_params=pltpu.CompilerParams(
+            collective_id=collective_id,
+            has_side_effects=True,
+            vmem_limit_bytes=67043328,
+            dimension_semantics=("arbitrary",),
+        ),
+        name="wide_grads",
+    )(at, *hidden, down)
 
 
 def solution(mesh):
@@ -474,45 +811,43 @@
         both = jnp.where(core == 0, jnp.concatenate([both, other], 2), jnp.concatenate([other, both], 2))
         downs = jnp.pad(w_down, ((0, 0), (0, f_own), (0, 0)))
         downs = jnp.where(core == 0, downs, jnp.roll(downs, f_own, 1))
-        weights = []
+        blocks = [[both[0, l : l + 1], both[1, l : l + 1], downs[l : l + 1]] for l in range(layers)]
+
+        def flat(full):
+            return [f.reshape(-1, f.shape[-1]) for f in full]
+
+        weights = [flat(gather(side, chips, splits, blocks[0], 1))]
+        hs, kept = [x], []
         for l in range(layers):
-            full = gather(side, chips, splits, [both[0, l : l + 1], both[1, l : l + 1], downs[l : l + 1]], 1)
-            weights.append([f.reshape(-1, f.shape[-1]) for f in full])
-
-        def forward(h, w):
-            a, scale = normed(h)
-            gate, up = dot(a, w[0]), dot(a, w[1])
-            return a, scale, gate, up, (jax.nn.silu(gate) * up).astype(BF16)
-
-        def backward(h, saved, w, g):
-            a, scale, gate, up, p = saved
-            dp = dot(g, w[2], ((1,), (1,))).astype(BF16).astype(F32)
-            sig = jax.nn.sigmoid(gate)
-            d_up = (dp * (gate * sig)).astype(BF16)
-            d_gate = (dp * up * (sig * (1 + gate * (1 - sig)))).astype(BF16)
-            down = dot(p, g, ((0,), (0,))).astype(BF16)
-            by_gate = dot(a, d_gate, ((0,), (0,))).astype(BF16)
-            by_up = dot(a, d_up, ((0,), (0,))).astype(BF16)
-            da = (
-                dot(d_gate, w[0], ((1,), (1,))).astype(BF16).astype(F32)
-                + dot(d_up, w[1], ((1,), (1,))).astype(BF16).astype(F32)
-            ).astype(BF16)
-            dh = (g.astype(F32) + norm_back(h, scale, da).astype(F32)).astype(BF16)
-            terms = [t.reshape(chips, -1, t.shape[-1]) for t in (by_gate, by_up, down)]
-            return dh, scatter(side, splits, terms, 2)
-
-        hs, saved = [x], []
-        for l in range(layers):
-            saved.append(forward(hs[l], weights[l]))
-            hs.append((hs[l].astype(F32) + dot(saved[l][4], weights[l][2]).astype(BF16).astype(F32)).astype(BF16))
-        g, sums = dy, [None] * layers
-        for l in reversed(range(layers)):
-            g, sums[l] = backward(hs[l], saved[l], weights[l], g)
-        mine = jnp.stack([jnp.stack([s[0], s[1]]) for s in sums], 1)
-        lower, upper = mine[:, :, :d_own], mine[:, :, d_own:]
-        got = lax.ppermute(jnp.where(core == 0, upper, lower), "dp", swap)
-        by = jnp.where(core == 0, jnp.concatenate([lower, got], -1), jnp.concatenate([got, upper], -1))
-        return g[None], by[0], by[1], jnp.stack([s[2] for s in sums])
+            if l < layers - 1:
+                h, saved, full = forward(side, chips, splits, hs[l], weights[l], blocks[l + 1], 3)
+                hs.append(h)
+                kept.append(saved)
+                weights.append(flat(full))
+
+        def tall(t):
+            return t.reshape(chips, -1, t.shape[-1])
+
+        def whole(mine):
+            lower, upper = mine[:, :d_own], mine[:, d_own:]
+            got = lax.ppermute(jnp.where(core == 0, upper, lower), "dp", swap)
+            return jnp.where(core == 0, jnp.concatenate([lower, got], -1), jnp.concatenate([got, upper], -1))
+
+        grads, g = top(hs[-1], dy, weights[-1])
+        by_gate, by_up, by_down = [], [], []
+        terms = [tall(t) for t in grads]
+        for l in reversed(range(layers - 1)):
+            down, g, hidden, done = lower(side, splits, kept[l][:2], hs[l], g, weights[l], terms, 4)
+            both = whole(jnp.stack(done[:2]))
+            by_gate.append(both[0])
+            by_up.append(both[1])
+            by_down.append(done[2])
+            done = wide_grads(side, chips, kept[l][2], hidden, tall(down), 2)
+            four = whole(jnp.stack(done[1:]))
+            by_gate.append(jnp.concatenate([four[0], four[1]], -1))
+            by_up.append(jnp.concatenate([four[2], four[3]], -1))
+            by_down.append(done[0])
+        return g[None], *(jnp.stack(t[::-1]) for t in (by_gate, by_up, by_down))
 
     wspec = P(None, "dp", None)
     out = P("rep", "dp", None)

time: 570 us -> 402 us (0.71); the launches traced: 561 us -> 402 us
  matrix products: 307 us -> 0 us
  Pallas kernels: 209 us -> 382 us
  local copies, waits for them, and re-layouts: 24.2 us -> 7.6 us
  other arithmetic: 15.1 us -> 4.93 us
    dot_general x17 -> x0, matrix products: 307 us -> none  [dot(): return lax.dot_general(a, w, (dims, ((), ())), preferred_element_type=F32)]
    pallas_call x2 -> x4, Pallas kernels: 118 us -> 336 us  [the longest x1 108 us: top(): pl.pallas_call(functools.partial(top_kernel, chunks, tiles), grid=(chunks...]
    pallas_call x2 -> x1, Pallas kernels: 91.3 us -> 46.2 us  [gather(): pl.pallas_call(functools.partial(gather_kernel, side, splits), out_shape=...]
    unnamed x45 -> x7, local copies, waits for them, and re-layouts: 20.4 us -> 3.86 us
  transfers between devices with their start and end apart: 2 -> 3, of which waited for: 0 -> 1; matrix products, arithmetic and copies ran while one was open for 8% -> 1% of each run, Pallas kernels for 0% -> 0%
where the time goes in v2:
time: 402 us
  Pallas kernels  382 us (95%)
  local copies, waits for them, and re-layouts  7.6 us (2%)
  starting transfers between devices  6.11 us (2%)
  other arithmetic  4.93 us (1%)
    pallas_call x1, Pallas kernels, top(): pl.pallas_call(functools.partial(top_kernel, chunks, tiles), grid=(chunks...  108 us
    pallas_call x1, Pallas kernels, lower(): pl.pallas_call(functools.partial(lower_kernel, side, splits, chunks, tile...  85.6 us
    pallas_call x1, Pallas kernels, wide_grads(): pl.pallas_call(functools.partial(wide_kernel, side), grid=(8 * PIECES + 1...  81.4 us
    pallas_call x1, Pallas kernels, forward(): pl.pallas_call(functools.partial(forward_kernel, side, splits, chunks, ti...  60.4 us
    pallas_call x1, Pallas kernels, gather(): pl.pallas_call(functools.partial(gather_kernel, side, splits), out_shape=...  46.2 us
  transfers between devices with their start and end apart: 3, of which 1 were waited for; matrix products, arithmetic and copies ran while one was open for 1% of the time, Pallas kernels for 0%

profile of v2, /device:TPU:97, one launch (start us, length us, event | category | flops | bytes accessed | tf_op | source)
XLA Modules:
  0.0 401.8 jit_solution(12258975844013095340)
XLA Ops:
  0.6 1.2 copy_bitcast_fusion
  1.8 0.1 pad_maximum_fusion
  1.9 0.6 copy.15
  2.5 2.1 collective-permute-start
  4.6 0.1 pad_select_fusion
  4.7 0.9 fusion.2
  5.6 0.7 collective-permute-done
  6.3 0.4 maximum_select_fusion
  6.7 1.0 slice_bitcast_fusion
  7.8 46.2 %gather.1 = (bf16[16,56,2560]{2,1,0:T(8,128)(2,1)}, bf16[16,56,2560]{2,1,0:T(8,128)(2,1)}, bf16[16,160,896]{2,1,0:T(8,128)(2,1)}) custom-call(bf16[1,56,2560]{2,1,0:T(8,128)(2,1)} %get-tuple-element.70.refs_0_, bf16[1,56,2560]{2,1,0:T(8,128)(2,1)} %get-tuple-element.69.refs_1_, bf16[1,160,896]{2,1,0:T(8,128)(2,1)} %get-tuple-element.72.refs_2_), custom_call_target="tpu_custom_call" | custom-call | tf_op jit(solution)/shard_map/gather/pallas_call | solution.py:229
  53.9 60.4 %forward.1 = (bf16[2048,896]{1,0:T(8,128)(2,1)}, f32[2048,2560]{1,0:T(8,128)}, f32[2048,2560]{1,0:T(8,128)}, bf16[896,2048]{1,0:T(8,128)(2,1)}, bf16[16,56,2560]...) custom-call(bf16[2048,896]{1,0:T(8,128)(2,1)} %bitcast.51, ...), custom_call_target="tpu_custom_call" | custom-call | tf_op jit(solution)/shard_map/forward/pallas_call | solution.py:546
  114.4 108.1 %top.1 = (bf16[896,2560]{1,0:T(8,128)(2,1)}, bf16[896,2560]{1,0:T(8,128)(2,1)}, bf16[2560,896]{1,0:T(8,128)(2,1)}, bf16[2048,896]{1,0:T(8,128)(2,1)}) custom-call(bf16[2048,896]{1,0:T(8,128)(2,1)} %get-tuple-element.33.h_ref, bf16[2048,896]{1,0:T(8,128)(2,1)} %bitcast.60, bf16[896,2560]{1,0:T(8,128)(2,1)} %bitcast.57, bf16[896,2560]{1,0:T(8,128)(2,1)} %bitcast.58, ...), custom_call_target="tpu_custom_call" | custom-call | tf_op jit(solution)/shard_map/top/pallas_call | solution.py:642
  222.5 85.6 %lower.1 = (bf16[2560,896]{1,0:T(8,128)(2,1)}, bf16[2048,896]{1,0:T(8,128)(2,1)}, bf16[2048,2560]{1,0:T(8,128)(2,1)}, bf16[2048,2560]{1,0:T(8,128)(2,1)}, bf16[5...) custom-call(bf16[2048,896]{1,0:T(8,128)(2,1)} %bitcast.52, ...), custom_call_target="tpu_custom_call" | custom-call | tf_op jit(solution)/shard_map/lower/pallas_call | solution.py:709
  308.1 81.4 %wide_grads.1 = (bf16[80,896]{1,0:T(8,128)(2,1)}, bf16[56,640]{1,0:T(8,128)(2,1)}, bf16[56,640]{1,0:T(8,128)(2,1)}, bf16[56,640]{1,0:T(8,128)(2,1)}, bf16[56,640]{1,0:T(8,128)(2,1)}) custom-call(bf16[896,2048]{1,0:T(8,128)(2,1)} %get-tuple-element.44.at_ref, bf16[2048,2560]{1,0:T(8,128)(2,1)} %get-tuple-element.45.dg_ref, ...), custom_call_target="tpu_custom_call" | custom-call | tf_op jit(solution)/shard_map/wide_grads/pallas_call | solution.py:772
  389.5 1.0 pad_maximum_fusion.3
  390.6 3.8 collective-permute-start.1
  394.4 1.2 broadcast_select_fusion
  395.7 0.1 collective-permute-start.2
  395.8 1.7 pad_maximum_fusion.4
  397.5 0.1 maximum_select_fusion.1
  397.7 0.1 maximum_select_fusion.2
  397.9 1.0 copy.19
  398.9 1.0 copy.18
  399.9 1.8 copy.23
  (14 shorter events, 0.3 us)
Async XLA Ops:
  0.6 4.0 copy-start.1
  2.5 3.7 collective-permute-start
  390.6 6.9 %collective-permute-start.1 = (bf16[4,28,640]{2,1,0:T(8,128)(2,1)S(1)}, bf16[4,28,640]{2,1,0:T(8,128)(2,1)S(1)}, u32[]{:S(2)}, u32[]{:S(2)}) collective-permute-start(bf16[4,28,640]{2,1,0:T(8,128)(2,1)S(1)} %get-tuple-element.80), channel_id=1, source_target_pairs={{0,1},{1,0},{2,3},{3,2},{4,5},{5,4},{6,7},{7,6},{8,9},{9,8},{10,11... | collective-permute-start | bytes 430088 | tf_op jit(solution)/shard_map/ppermute | solution.py:833
  394.4 5.5 %copy-start = (bf16[2048,896]{1,0:T(8,128)(2,1)S(1)}, bf16[2048,896]{1,0:T(8,128)(2,1)}, u32[]{:S(2)}) copy-start(bf16[2048,896]{1,0:T(8,128)(2,1)} %get-tuple-element.43) | copy-start | bytes 11010052
  395.7 2.0 collective-permute-start.2
